TPU v7x, 32 devices: a whole 2x2x4 slice. The times are simulated.
32 devices in a mesh: band: 8 (over z, x), slab: 4 (over y, core).
Axes of the slice: x: 2, y: 2, z: 4, core: 2. Of those that a mesh axis runs over, the one named last changes fastest.
Arguments:
- orbitals: float32 [512, 64, 512], P('band', 'slab'), may hold values from -6 to 6
- potential: float32 [64, 512], P('slab'), may hold values from 0 to 1
- projectors: float32 [4, 2048, 128], replicated, may hold values from -0.125 to 0.125
- atom_kind: int32 [32], P('slab'), may hold values from 0 to 3
- atom_plane: int32 [32], P('slab'), may hold values from 0 to 60, as said below
- atom_coef: float32 [32, 128], P('slab'), may hold values from 0.2 to 1
- filter_cut: float32 [1], replicated, may hold values from 0.5 to 2
- filter_top: float32 [1], replicated, may hold values from 9 to 14
Outputs:
- new_orbitals: float32 [512, 32768], P(None, ('slab', 'band'))
Inputs may be any that keep to these rules, and one draw needn't show every extreme that they name: `atom_plane`: block i's 4 planes lie inside the slab of planes (i // 8) * 16 to (i // 8 + 1) * 16 - 1; blocks may share planes.
All inputs are finite; a program needn't handle non-finite values.
Results may differ from a plain program's by a relative error of at most 0.0003.
Values sent between devices are 32-bit elements; how exact they have to be, the bound alone decides.
A program may use at most 128 MiB of HBM per device.

v0:
```python
import functools

import jax
import jax.numpy as jnp
from jax import lax
from jax.experimental import pallas as pl
from jax.experimental.pallas import tpu as pltpu
from jax.sharding import PartitionSpec as P

GZ = 32
ORDER = 6

low_edge = -1.0
highest = lax.Precision.HIGHEST
f32 = jnp.float32
bf16 = jnp.bfloat16


def transverse_matrix(points, width_z):
    r = jnp.arange(points)
    y, z = r // width_z, r % width_z
    dy = jnp.abs(y[:, None] - y[None, :])
    dz = jnp.abs(z[:, None] - z[None, :])
    line = lambda d: jnp.where(d == 0, -30.0, jnp.where(d == 1, 16.0, jnp.where(d == 2, -1.0, 0.0)))
    return (jnp.where(dz == 0, line(dy), 0.0) + jnp.where(dy == 0, line(dz), 0.0)).astype(bf16)


def filter_kernel(
    plane_ref, kind_ref, scal_ref, orb_ref, pot_ref, coef_ref, lap_ref, proj_ref,
    out_ref, ph_ref, pl_ref, buf, split, trans, spread, halo, send_sem, recv_sem,
):
    planes, rows, points = orb_ref.shape
    atoms = coef_ref.shape[0]
    depth = proj_ref.shape[1]
    size = lax.axis_size("slab")
    me = lax.axis_index("slab")
    right, left = lax.rem(me + 1, size), lax.rem(me + size - 1, size)

    barrier = pltpu.get_barrier_semaphore()
    for neighbour in (left, right):
        pl.semaphore_signal(barrier, inc=1, device_id={"slab": neighbour}, device_id_type=pl.DeviceIdType.MESH)
    pl.semaphore_wait(barrier, 2)

    buf[0] = orb_ref[...]
    buf[1] = jnp.zeros((planes, rows, points), f32)
    for a in range(atoms):
        spread[a, 0] = jnp.zeros((rows, points), f32)
        spread[a, depth + 1] = jnp.zeros((rows, points), f32)
    for k in range(proj_ref.shape[0]):
        for j in range(depth):
            table = proj_ref[k, j]
            high = table.astype(bf16)
            ph_ref[k, j] = high
            pl_ref[k, j] = (table - high.astype(f32)).astype(bf16)
    centre = scal_ref[2 * ORDER]

    def step(s, carry):
        cur = lax.rem(s, 2)
        nxt = 1 - cur
        scale = scal_ref[2 * s]
        back = scal_ref[2 * s + 1]
        copies = []
        for side, first, target in ((0, planes - 2, right), (1, 0, left)):
            copy = pltpu.make_async_remote_copy(
                src_ref=buf.at[cur, pl.ds(first, 2)],
                dst_ref=halo.at[s, side],
                send_sem=send_sem.at[side],
                recv_sem=recv_sem.at[s, side],
                device_id={"slab": target},
                device_id_type=pl.DeviceIdType.MESH,
            )
            copy.start()
            copies.append(copy)

        group = 4 if planes % 4 == 0 else 1

        def lap_group(g, c):
            x0 = g * group
            f = buf[cur, pl.ds(x0, group)]
            hi = f.astype(bf16)
            lo = (f - hi.astype(f32)).astype(bf16)
            both = jnp.concatenate([hi, lo], axis=1)
            split[pl.ds(x0, group)] = both
            r = jnp.dot(both.reshape(group * 2 * rows, points), lap_ref[...], preferred_element_type=f32)
            r = r.reshape(group, 2 * rows, points)
            trans[pl.ds(x0, group)] = r[:, :rows] + r[:, rows:]
            return c

        lax.fori_loop(0, planes // group, lap_group, 0)

        def atom(a, c):
            p = plane_ref[a]
            k = kind_ref[a]
            coupled = jnp.zeros((rows, ph_ref.shape[3]), f32)
            for j in range(depth):
                both = split[p + j]
                r = jnp.dot(both, ph_ref[k, j], preferred_element_type=f32)
                e = jnp.dot(both[:rows], pl_ref[k, j], preferred_element_type=f32)
                coupled = coupled + (r[:rows] + (r[rows:] + e))
            coupled = coupled * coef_ref[a]
            hi = coupled.astype(bf16)
            lo = (coupled - hi.astype(f32)).astype(bf16)
            both = jnp.concatenate([hi, lo], axis=0)
            nt = (((1,), (1,)), ((), ()))
            for j in range(depth):
                r = lax.dot_general(both, ph_ref[k, j], nt, preferred_element_type=f32)
                e = lax.dot_general(hi, pl_ref[k, j], nt, preferred_element_type=f32)
                spread[a, j + 1] = r[:rows] + (r[rows:] + e)
            return c

        lax.fori_loop(0, atoms, atom, 0)

        piece = 16 if rows % 16 == 0 else 8

        def plane(x, sources):
            slots = [jnp.clip(x - plane_ref[a], -1, depth) + 1 for a in range(atoms)]
            for r0 in range(0, rows, piece):
                rs = pl.ds(r0, piece)
                f = buf[cur, x, rs]
                m2, m1, p1, p2 = [ref[index + (rs,)] for ref, index in sources]
                total = trans[x, rs] * (-0.5 / 12.0) + (pot_ref[x] + (1.25 - centre)) * f
                total = total + (m1 + p1) * (-2.0 / 3.0) + (m2 + p2) * (1.0 / 24.0)
                for a in range(atoms):
                    total = total + spread[a, slots[a], rs]
                buf[nxt, x, rs] = scale * total - back * buf[nxt, x, rs]

        def interior(x, c):
            plane(x, [(buf, (cur, x + d)) for d in (-2, -1, 1, 2)])
            return c

        lax.fori_loop(2, planes - 2, interior, 0)
        for copy in copies:
            copy.wait()

        def source(x):
            if x < 0:
                return halo, (s, 0, x + 2)
            if x >= planes:
                return halo, (s, 1, x - planes)
            return buf, (cur, x)

        for x in (0, 1, planes - 2, planes - 1):
            plane(x, [source(x + d) for d in (-2, -1, 1, 2)])
        return carry

    lax.fori_loop(0, ORDER, step, 0)
    width = out_ref.shape[2]
    unit = min(width, points)
    for start in range(0, planes * points, unit):
        x, at = start // points, start % points
        chunk, lane = start // width, start % width
        out_ref[chunk, :, lane : lane + unit] = buf[ORDER % 2, x, :, at : at + unit]


def filter_call(plane, kind, scal, orb, pot, coef, lap, tables, chunks):
    planes, rows, points = orb.shape
    atoms = coef.shape[0]
    depth = tables.shape[1]
    smem = pl.BlockSpec(memory_space=pltpu.SMEM)
    vmem = pl.BlockSpec(memory_space=pltpu.VMEM)
    return pl.pallas_call(
        filter_kernel,
        out_shape=jax.ShapeDtypeStruct((chunks, rows, planes * points // chunks), f32),
        in_specs=[smem] * 3 + [vmem] * 5,
        out_specs=vmem,
        scratch_shapes=[
            pltpu.VMEM(tables.shape, bf16),
            pltpu.VMEM(tables.shape, bf16),
            pltpu.VMEM((2, planes, rows, points), f32),
            pltpu.VMEM((planes, 2 * rows, points), bf16),
            pltpu.VMEM((planes, rows, points), f32),
            pltpu.VMEM((atoms, depth + 2, rows, points), f32),
            pltpu.VMEM((ORDER, 2, 2, rows, points), f32),
            pltpu.SemaphoreType.DMA((2,)),
            pltpu.SemaphoreType.DMA((ORDER, 2)),
        ],
        compiler_params=pltpu.CompilerParams(
            collective_id=0, has_side_effects=True, vmem_limit_bytes=56 * 1024 * 1024
        ),
        name="cheb_filter",
    )(plane, kind, scal, orb, pot, coef, lap, tables)


def factor_kernel(nb, g_ref, w_ref, a_ref, d_ref):
    n = w_ref.shape[0]
    a_ref[...] = jnp.zeros((n, n), f32)
    at = 0
    for i in range(n // nb):
        for j in range(i + 1):
            a_ref[i * nb : (i + 1) * nb, j * nb : (j + 1) * nb] = g_ref[at : at + nb]
            at += nb
    w_ref[...] = jnp.zeros((n, n), f32)
    rows = lax.broadcasted_iota(jnp.int32, (nb, nb), 0)
    cols = lax.broadcasted_iota(jnp.int32, (nb, nb), 1)
    row_ids = lax.broadcasted_iota(jnp.int32, (nb, 1), 0)
    lane_ids = lax.broadcasted_iota(jnp.int32, (1, nb), 1)
    nt = (((1,), (1,)), ((), ()))
    for b in range(n // nb):
        lo, hi = b * nb, (b + 1) * nb
        d_ref[:, :nb] = a_ref[lo:hi, lo:hi]
        d_ref[:, nb:] = (rows == cols).astype(f32)

        def eliminate(t, c):
            k = 2 * t
            top = d_ref[pl.ds(k, 1), :]
            low = d_ref[pl.ds(k + 1, 1), :]
            block = d_ref[:, :nb]

            def lane(row, at):
                return jnp.sum(jnp.where(lane_ids == at, row[:, :nb], 0.0), axis=1, keepdims=True)

            def column(at):
                return jnp.sum(jnp.where(cols == at, block, 0.0), axis=1, keepdims=True)

            p11, p12, p22 = lane(top, k), lane(top, k + 1), lane(low, k + 1)
            c0, c1 = column(k), column(k + 1)
            inv1 = 1.0 / p11
            link = p12 * inv1
            inv2 = 1.0 / (p22 - p12 * link)
            low = (low - link * top) * inv2
            c1 = jnp.where(row_ids > k + 1, c1 - link * c0, 0.0)
            c0 = jnp.where(row_ids > k, c0, 0.0)
            d_ref[...] = d_ref[...] - c0 * (top * inv1) - c1 * low
            return c

        lax.fori_loop(0, nb // 2, eliminate, 0)
        pivots = jnp.sum(jnp.where(rows == cols, d_ref[:, :nb], 0.0), axis=1, keepdims=True)
        inverse = d_ref[:, nb:] / jnp.sqrt(pivots)
        w_ref[lo:hi, lo:hi] = inverse
        if lo > 0:
            mixed = jnp.dot(a_ref[lo:hi, :lo], w_ref[:lo, :lo], precision=highest, preferred_element_type=f32)
            w_ref[lo:hi, :lo] = -jnp.dot(inverse, mixed, precision=highest, preferred_element_type=f32)
        if hi < n:
            panel = lax.dot_general(a_ref[hi:, lo:hi], inverse, nt, precision=highest, preferred_element_type=f32)
            a_ref[hi:, lo:hi] = panel
            a_ref[hi:, hi:] = a_ref[hi:, hi:] - lax.dot_general(
                panel, panel, nt, precision=highest, preferred_element_type=f32
            )


def inverse_factor(blocks, n):
    nb = block_size(n)
    vmem = pl.BlockSpec(memory_space=pltpu.VMEM)
    return pl.pallas_call(
        functools.partial(factor_kernel, nb),
        out_shape=jax.ShapeDtypeStruct((n, n), f32),
        in_specs=[vmem],
        out_specs=vmem,
        scratch_shapes=[pltpu.VMEM((n, n), f32), pltpu.VMEM((nb, 2 * nb), f32)],
        compiler_params=pltpu.CompilerParams(vmem_limit_bytes=32 * 1024 * 1024),
        name="factor_inverse",
    )(blocks)


def reduce_kernel(nb, g_ref, out_ref, pack, first, part, second, full, sends, recvs_a, recvs_b, recvs_c, recvs_d):
    n = g_ref.shape[0]
    total = pack.shape[0]
    slabs, bands = lax.axis_size("slab"), lax.axis_size("band")
    my_slab, my_band = lax.axis_index("slab"), lax.axis_index("band")
    deep, thin = total // slabs, total // slabs // bands
    at = 0
    for i in range(n // nb):
        for j in range(i + 1):
            pack[at : at + nb] = g_ref[i * nb : (i + 1) * nb, j * nb : (j + 1) * nb]
            at += nb
    if at < total:
        pack[at:] = jnp.zeros((total - at, nb), f32)

    def peer(me, size, d):
        return lax.rem(me + d, size)

    barrier = pltpu.get_barrier_semaphore()
    for axis, me, size in (("slab", my_slab, slabs), ("band", my_band, bands)):
        for d in range(1, size):
            pl.semaphore_signal(
                barrier, inc=1, device_id={axis: peer(me, size, d)}, device_id_type=pl.DeviceIdType.MESH
            )
    pl.semaphore_wait(barrier, slabs + bands - 2)

    def exchange(axis, me, size, source, target, recvs):
        copies = []
        for d in range(1, size):
            other = peer(me, size, d)
            copies.append(
                pltpu.make_async_remote_copy(
                    src_ref=source(other),
                    dst_ref=target(d),
                    send_sem=sends.at[d - 1],
                    recv_sem=recvs.at[d - 1],
                    device_id={axis: other},
                    device_id_type=pl.DeviceIdType.MESH,
                )
            )
        for copy in copies:
            copy.start()
        for copy in copies:
            copy.wait()

    def span(start, length):
        return pl.ds(pl.multiple_of(start, 8), length)

    exchange(
        "slab", my_slab, slabs, lambda t: pack.at[span(t * deep, deep)], lambda d: first.at[d - 1], recvs_a
    )
    value = pack[span(my_slab * deep, deep)]
    for d in range(1, slabs):
        value = value + first[d - 1]
    part[...] = value
    exchange(
        "band", my_band, bands, lambda t: part.at[span(t * thin, thin)], lambda d: second.at[d - 1], recvs_b
    )
    value = part[span(my_band * thin, thin)]
    for d in range(1, bands):
        value = value + second[d - 1]
    mine = span(my_slab * deep + my_band * thin, thin)
    full[mine] = value
    exchange("band", my_band, bands, lambda t: full.at[mine], lambda d: full.at[mine], recvs_c)
    mine_deep = span(my_slab * deep, deep)
    exchange("slab", my_slab, slabs, lambda t: full.at[mine_deep], lambda d: full.at[mine_deep], recvs_d)
    out_ref[...] = full[...]


def block_size(n):
    return 128 if n % 128 == 0 else n


def reduced_blocks(gram):
    n = gram.shape[0]
    nb = block_size(n)
    slabs, bands = lax.axis_size("slab"), lax.axis_size("band")
    count = n // nb
    used = count * (count + 1) // 2 * nb
    unit = 8 * slabs * bands
    total = (used + unit - 1) // unit * unit
    vmem = pl.BlockSpec(memory_space=pltpu.VMEM)
    dma = pltpu.SemaphoreType.DMA
    return pl.pallas_call(
        functools.partial(reduce_kernel, nb),
        out_shape=jax.ShapeDtypeStruct((total, nb), f32),
        in_specs=[vmem],
        out_specs=vmem,
        scratch_shapes=[
            pltpu.VMEM((total, nb), f32),
            pltpu.VMEM((slabs - 1, total // slabs, nb), f32),
            pltpu.VMEM((total // slabs, nb), f32),
            pltpu.VMEM((bands - 1, total // slabs // bands, nb), f32),
            pltpu.VMEM((total, nb), f32),
            dma((max(slabs, bands) - 1,)),
            dma((slabs - 1,)),
            dma((bands - 1,)),
            dma((bands - 1,)),
            dma((slabs - 1,)),
        ],
        compiler_params=pltpu.CompilerParams(
            collective_id=1, has_side_effects=True, vmem_limit_bytes=32 * 1024 * 1024
        ),
        name="gram_sum",
    )(gram)


def local(
    orbitals, potential, projectors, atom_kind, atom_plane, atom_coef, filter_cut, filter_top
):
    band_count, planes, points = orbitals.shape
    kind_count, block_pts, func_count = projectors.shape
    atom_count = atom_kind.shape[0]
    depth = block_pts // points
    bands = lax.axis_size("band")
    local_plane = (atom_plane - lax.axis_index("slab") * planes).astype(jnp.int32)

    cut_value = filter_cut[0]
    top_value = filter_top[0]
    half_width = (top_value - cut_value) / 2.0
    centre = (top_value + cut_value) / 2.0
    sigma_now = half_width / (low_edge - centre)
    tau_value = 2.0 / sigma_now
    scal = [sigma_now / half_width, jnp.zeros((), f32)]
    for _ in range(ORDER - 1):
        sigma_next = 1.0 / (tau_value - sigma_now)
        scal += [2.0 * sigma_next / half_width, sigma_now * sigma_next]
        sigma_now = sigma_next
    scal = jnp.stack(scal + [centre])

    tables = projectors.reshape(kind_count, depth, points, func_count)
    filtered = filter_call(
        local_plane, atom_kind, scal,
        jnp.transpose(orbitals, (1, 0, 2)), potential.reshape(planes, 1, points),
        atom_coef.reshape(atom_count, 1, func_count), transverse_matrix(points, GZ), tables, bands,
    )
    grid_layout = lax.all_to_all(filtered, "band", split_axis=0, concat_axis=0, tiled=True)
    grid_layout = grid_layout.reshape(bands * band_count, planes * points // bands)
    point_total = grid_layout.shape[1] * lax.axis_size(("band", "slab"))
    gram = jnp.dot(grid_layout, grid_layout.T, precision=highest) / point_total
    factor_inverse = inverse_factor(reduced_blocks(gram), gram.shape[0])
    return jnp.dot(factor_inverse, grid_layout, precision=lax.Precision.HIGH)


def solution(mesh):
    in_specs = (
        P("band", "slab", None),
        P("slab", None),
        P(),
        P("slab"),
        P("slab"),
        P("slab", None),
        P(),
        P(),
    )
    out_specs = P(None, ("slab", "band"))
    return jax.shard_map(local, mesh=mesh, in_specs=in_specs, out_specs=out_specs, check_vma=False)
```

profile of v0, /device:TPU:1, one launch (start us, length us, event | category | flops | bytes accessed | tf_op | source)
XLA Modules:
  0.0 202.8 jit_solution(9125169677745095523)
XLA Ops:
  1.9 1.4 reshape.65.pot_ref
  3.2 0.0 copy-start
  3.2 4.1 %copy.11 = f32[64,16,512]{2,0,1:T(8,128)} copy(f32[64,16,512]{2,1,0:T(8,128)} %param.8) | data formatting | bytes 4194304 | tf_op args[0]
  7.4 0.0 copy-done
  7.4 0.6 broadcast_subtract_fusion.plane_ref
  8.0 1.7 add_convert_fusion.lap_ref
  9.6 0.7 stack.48.scal_ref
  10.3 67.7 %cheb_filter.1 = f32[8,64,1024]{2,1,0:T(8,128)} custom-call(s32[8]{0:T(128)} %broadcast_subtract_fusion.plane_ref, s32[8]{0:T(128)} %kind_ref.1, f32[13]{0:T(128)} %stack.48.scal_ref, f32[16,64,512]{2,1,0:T(8,128)} %bitcast.25, f32[16,1,512]{2,1,0:T(1,128)} %reshape.65.pot_ref, f32[8,1,128]{2,1,0:T(1,128)} %bitcast.27, ...), custom_call_target="tpu_custom_call" | custom-call | tf_op jit(solution)/shard_map/cheb_filter/pallas_call | solution.py:161
  78.0 53.7 %all_to_all.5 = f32[8,64,1024]{2,1,0:T(8,128)S(1)} all-to-all(f32[8,64,1024]{2,1,0:T(8,128)} %cheb_filter.1), channel_id=1, replica_groups=mesh['band'=8,'slab'=4] {'band'}, dimensions={0} | all-to-all | bytes 4194304 | tf_op jit(solution)/shard_map/all_to_all | solution.py:390
  131.7 3.5 %convolution_multiply_fusion.g_ref = f32[512,512]{1,0:T(8,128)S(1)} fusion(f32[512,1024]{1,0:T(8,128)S(1)} %bitcast.23), kind=kOutput, calls=%fused_computation.1 | convolution fusion | flops 3221487616 | bytes 3145728 | tf_op jit(solution)/shard_map/dot_general | solution.py:393
  135.2 28.8 %gram_sum.1.g_ref = f32[1280,128]{1,0:T(8,128)S(1)} custom-call(f32[512,512]{1,0:T(8,128)S(1)} %convolution_multiply_fusion.g_ref), custom_call_target="tpu_custom_call" | custom-call | tf_op jit(solution)/shard_map/gram_sum/pallas_call | solution.py:337
  164.0 35.6 %factor_inverse.1 = f32[512,512]{1,0:T(8,128)S(1)} custom-call(f32[1280,128]{1,0:T(8,128)S(1)} %gram_sum.1.g_ref), custom_call_target="tpu_custom_call" | custom-call | tf_op jit(solution)/shard_map/factor_inverse/pallas_call | solution.py:244
  199.6 3.2 %fusion.11 = f32[512,1024]{1,0:T(8,128)} fusion(f32[512,512]{1,0:T(8,128)S(1)} %factor_inverse.1, f32[512,1024]{1,0:T(8,128)S(1)} %bitcast.24), kind=kOutput, calls=%fused_computation.22 | convolution fusion | flops 1610612736 | bytes 5242880 | tf_op jit(solution)/shard_map/dot_general | solution.py:395
  (1 shorter events, 0.0 us)
Async XLA Ops:
  3.2 4.1 %copy-start = (s32[8]{0:T(128)S(1)}, s32[8]{0:T(128)}, u32[]{:S(2)}) copy-start(s32[8]{0:T(128)} %param.12) | copy-start | bytes 100
where the time goes:
time: 203 us
  Pallas kernels  132 us (65%)
  blocking collectives  53.7 us (26%)
  matrix products  6.69 us (3%)
  local copies, waits for them, and re-layouts  6.21 us (3%)
  other arithmetic  2.25 us (1%)
    pallas_call x1, Pallas kernels, filter_call(): pl.pallas_call(filter_kernel, out_shape=jax.ShapeDtypeStruct((chunks, row...  67.7 us
    all_to_all x1, blocking collectives, local(): lax.all_to_all(filtered, 'band', split_axis=0, concat_axis=0, tiled=True)  53.7 us
    pallas_call x1, Pallas kernels, inverse_factor(): pl.pallas_call(functools.partial(factor_kernel, nb), out_shape=jax.ShapeD...  35.6 us
    pallas_call x1, Pallas kernels, reduced_blocks(): pl.pallas_call(functools.partial(reduce_kernel, nb), out_shape=jax.ShapeD...  28.8 us
    unnamed x3, local copies, waits for them, and re-layouts  4.14 us

commit v1 on v0

v1 whole, which is shorter than its diff:
```python
import functools
import jax
import jax.numpy as jnp
from jax import lax
from jax.experimental import pallas as pl
from jax.experimental.pallas import tpu as pltpu
from jax.sharding import PartitionSpec as P

GZ = 32
ORDER = 6

low_edge = -1.0
highest = lax.Precision.HIGHEST
f32 = jnp.float32
bf16 = jnp.bfloat16
MESH = pl.DeviceIdType.MESH


def halves(value):
    high = value.astype(bf16)
    return high, (value - high.astype(f32)).astype(bf16)


def chebyshev_scalars(cut, top):
    half = (top - cut) / 2.0
    centre = (top + cut) / 2.0
    sigma = half / (low_edge - centre)
    tau = 2.0 / sigma
    pairs = [(sigma / half, None)]
    for _ in range(ORDER - 1):
        following = 1.0 / (tau - sigma)
        pairs.append((2.0 * following / half, sigma * following))
        sigma = following
    return centre, pairs


def filter_kernel(
    groups, plane_ref, kind_ref, scal_ref, orb_ref, pot_ref, coef_ref, proj_ref,
    out_ref, table, back, lap, even, odd, split, spread, halo, raw, load_sem, table_sem, own_sem,
    send_sem, recv_sem, out_sem, in_sem,
):
    rows, planes, points = orb_ref.shape
    kinds, block, funcs = proj_ref.shape
    atoms = coef_ref.shape[0]
    depth = block // points
    share = rows // groups
    width = out_ref.shape[2]
    slabs, bands = lax.axis_size("slab"), lax.axis_size("band")
    me, my_band = lax.axis_index("slab"), lax.axis_index("band")
    right, left = lax.rem(me + 1, slabs), lax.rem(me + slabs - 1, slabs)

    loads = []
    for x in range(planes):
        loads.append(pltpu.make_async_copy(orb_ref.at[:, x], even.at[x], load_sem.at[x]))
        loads[-1].start()
    tables = []
    for k in range(kinds):
        tables.append(pltpu.make_async_copy(proj_ref.at[k], raw.at[k], table_sem.at[k]))
        tables[-1].start()

    barrier = pltpu.get_barrier_semaphore()
    for neighbour in (left, right):
        pl.semaphore_signal(barrier, inc=1, device_id={"slab": neighbour}, device_id_type=MESH)
    for d in range(1, bands):
        pl.semaphore_signal(barrier, inc=1, device_id={"band": lax.rem(my_band + d, bands)}, device_id_type=MESH)
    pl.semaphore_wait(barrier, bands + 1)

    zeros = jnp.zeros((rows, points), f32)

    def clear(x, c):
        odd[x] = zeros
        return c

    lax.fori_loop(0, planes, clear, 0)

    def clear_spread(a, c):
        spread[a, 0] = zeros[:share]
        spread[a, depth + 1] = zeros[:share]
        return c

    lax.fori_loop(0, atoms, clear_spread, 0)

    strip = 64

    def lap_rows(i, c):
        r = lax.broadcasted_iota(jnp.int32, (strip, points), 0) + i * strip
        q = lax.broadcasted_iota(jnp.int32, (strip, points), 1)
        dy = jnp.abs(r // GZ - q // GZ)
        dz = jnp.abs(r % GZ - q % GZ)

        def line(d):
            return jnp.where(d == 0, -30.0, jnp.where(d == 1, 16.0, jnp.where(d == 2, -1.0, 0.0)))

        lap[pl.ds(i * strip, strip)] = (jnp.where(dz == 0, line(dy), 0.0) + jnp.where(dy == 0, line(dz), 0.0)).astype(bf16)
        return c

    lax.fori_loop(0, points // strip, lap_rows, 0)

    part = 256

    for k in range(kinds):
        tables[k].wait()

        def convert(i, c):
            at = pl.ds(i * part, part)
            high, low = halves(raw[k, at])
            table[k, at, :funcs] = high
            table[k, at, funcs:] = low
            lanes = pl.ds(pl.multiple_of(i * part, part), part)
            back[k, :funcs, lanes] = high.T
            back[k, funcs:, lanes] = low.T
            return c

        lax.fori_loop(0, block // part, convert, 0)

    for copy in loads:
        copy.wait()

    centre = scal_ref[2 * ORDER]
    quad = 4
    places = [plane_ref[a] - me * planes for a in range(atoms)]
    order = sorted(range(1, bands), key=lambda d: abs(d - bands / 2))
    unit = min(width, points)
    units = width // unit

    def outgoing(g, d, u):
        rs = pl.ds(pl.multiple_of(g * share, share), share)
        target = lax.rem(my_band + d, bands)
        if width >= points:
            src = even.at[target * units + u, rs]
        else:
            per = points // width
            src = even.at[target // per, rs, pl.ds(pl.multiple_of(lax.rem(target, per) * width, 128), width)]
        return pltpu.make_async_remote_copy(
            src_ref=src,
            dst_ref=out_ref.at[my_band, rs, u * unit : (u + 1) * unit],
            send_sem=out_sem.at[g, d - 1, u],
            recv_sem=in_sem.at[g, d - 1, u],
            device_id={"band": target},
            device_id_type=MESH,
        )

    def own(u):
        if width >= points:
            src = even.at[my_band * units + u]
        else:
            per = points // width
            src = even.at[my_band // per, :, pl.ds(pl.multiple_of(lax.rem(my_band, per) * width, 128), width)]
        return pltpu.make_async_copy(src, out_ref.at[my_band, :, u * unit : (u + 1) * unit], own_sem.at[u])

    def group_step(g, first):
        rs = pl.ds(first, share)

        def split_plane(x, c):
            high, low = halves(even[x, rs])
            split[x, :share] = high
            split[x, share:] = low
            return c

        lax.fori_loop(0, planes, split_plane, 0)

        def step(s, cur, nxt):
            scale = scal_ref[2 * s]
            pull = scal_ref[2 * s + 1]
            copies = []
            for side, start, target in ((0, planes - 2, right), (1, 0, left)):
                copy = pltpu.make_async_remote_copy(
                    src_ref=cur.at[pl.ds(start, 2), rs],
                    dst_ref=halo.at[g, s, side],
                    send_sem=send_sem.at[side],
                    recv_sem=recv_sem.at[g, s, side],
                    device_id={"slab": target},
                    device_id_type=MESH,
                )
                copy.start()
                copies.append(copy)

            def atom(a, c):
                p = jnp.clip(plane_ref[a] - me * planes, 0, planes - depth)
                k = kind_ref[a]
                both = jnp.concatenate([split[p + j] for j in range(depth)], axis=1)
                r = jnp.dot(both, table[k], preferred_element_type=f32)
                coupled = r[:share, :funcs] + (r[:share, funcs:] + r[share:, :funcs])
                high, low = halves(coupled * coef_ref[pl.ds(a, 1)])
                pair = jnp.concatenate(
                    [jnp.concatenate([high, high], axis=1), jnp.concatenate([low, low], axis=1)], axis=0
                )
                for j in range(depth):
                    r = jnp.dot(pair, back[k, :, j * points : (j + 1) * points], preferred_element_type=f32)
                    spread[a, j + 1] = r[:share] + r[share:]
                return c

            lax.fori_loop(0, atoms, atom, 0, unroll=True)

            slots = {x: [jnp.clip(x - places[a], -1, depth) + 1 for a in range(atoms)] for x in range(planes)}

            def quads(xs, take):
                both = jnp.concatenate([split[x] for x in xs], axis=0)
                r = jnp.dot(both, lap[...], preferred_element_type=f32)
                piece = min(16, share)
                span = min(256, points)
                for r0, l0 in [(r0, l0) for r0 in range(0, share, piece) for l0 in range(0, points, span)]:
                    ls = slice(l0, l0 + span)
                    fs = {}
                    for x in xs:
                        for d in (-2, -1, 0, 1, 2):
                            if x + d not in fs:
                                fs[x + d] = take(x + d, r0, piece, ls)
                    for i, x in enumerate(xs):
                        base = i * 2 * share + r0
                        total = (r[base : base + piece, ls] + r[base + share : base + share + piece, ls]) * (-0.5 / 12.0)
                        total = total + (pot_ref[pl.ds(x, 1), ls] + (1.25 - centre)) * fs[x]
                        total = total + (fs[x - 1] + fs[x + 1]) * (-2.0 / 3.0) + (fs[x - 2] + fs[x + 2]) * (1.0 / 24.0)
                        for a in range(atoms):
                            total = total + spread[a, slots[x][a], r0 : r0 + piece, ls]
                        at = (x, pl.ds(first + r0, piece), ls)
                        fresh = scale * total - pull * nxt[at]
                        nxt[at] = fresh
                        high, low = halves(fresh)
                        split[x, r0 : r0 + piece, ls] = high
                        split[x, share + r0 : share + r0 + piece, ls] = low

            def take(x, r0, piece, ls):
                if x < 0:
                    return halo[g, s, 0, x + 2, r0 : r0 + piece, ls]
                if x >= planes:
                    return halo[g, s, 1, x - planes, r0 : r0 + piece, ls]
                return cur[x, pl.ds(first + r0, piece), ls]

            for x0 in range(2, planes - 2, quad):
                quads(list(range(x0, min(x0 + quad, planes - 2))), take)
            for copy in copies:
                copy.wait()
            quads([0, 1, planes - 2, planes - 1], take)

        def two(i, c):
            step(2 * i, even, odd)
            step(2 * i + 1, odd, even)
            return c

        lax.fori_loop(0, ORDER // 2, two, 0)

    def run_group(g, c):
        group_step(g, pl.multiple_of(g * share, share))
        for d in order:
            for u in range(units):
                outgoing(g, d, u).start()
        return c

    lax.fori_loop(0, groups, run_group, 0)
    for u in range(units):
        own(u).start()
    for g in range(groups):
        for d in order:
            for u in range(units):
                outgoing(g, d, u).wait()
    for u in range(units):
        own(u).wait()


def filter_call(plane, kind, scal, orb, pot, coef, proj, groups):
    rows, planes, points = orb.shape
    atoms = coef.shape[0]
    kinds, block, funcs = proj.shape
    depth = block // points
    bands = lax.axis_size("band")
    share = rows // groups
    width = planes * points // bands
    units = max(width // points, 1)
    smem = pl.BlockSpec(memory_space=pltpu.SMEM)
    vmem = pl.BlockSpec(memory_space=pltpu.VMEM)
    hbm = pl.BlockSpec(memory_space=pl.ANY)
    dma = pltpu.SemaphoreType.DMA
    return pl.pallas_call(
        functools.partial(filter_kernel, groups),
        out_shape=jax.ShapeDtypeStruct((bands, rows, planes * points // bands), f32),
        in_specs=[smem] * 3 + [hbm, vmem, vmem, hbm],
        out_specs=vmem,
        scratch_shapes=[
            pltpu.VMEM((kinds, block, 2 * funcs), bf16),
            pltpu.VMEM((kinds, 2 * funcs, block), bf16),
            pltpu.VMEM((points, points), bf16),
            pltpu.VMEM((planes, rows, points), f32),
            pltpu.VMEM((planes, rows, points), f32),
            pltpu.VMEM((planes, 2 * share, points), bf16),
            pltpu.VMEM((atoms, depth + 2, share, points), f32),
            pltpu.VMEM((groups, ORDER, 2, 2, share, points), f32),
            pltpu.VMEM((kinds, block, funcs), f32),
            dma((planes,)),
            dma((kinds,)),
            dma((units,)),
            dma((2,)),
            dma((groups, ORDER, 2)),
            dma((groups, bands - 1, units)),
            dma((groups, bands - 1, units)),
        ],
        compiler_params=pltpu.CompilerParams(
            collective_id=0, has_side_effects=True, vmem_limit_bytes=60 * 1024 * 1024
        ),
        name="cheb_filter",
    )(plane, kind, scal, orb, pot, coef, proj)


def factor_kernel(nb, g_ref, w_ref, a_ref, d_ref):
    n = w_ref.shape[0]
    a_ref[...] = jnp.zeros((n, n), f32)
    at = 0
    for i in range(n // nb):
        for j in range(i + 1):
            a_ref[i * nb : (i + 1) * nb, j * nb : (j + 1) * nb] = g_ref[at : at + nb]
            at += nb
    w_ref[...] = jnp.zeros((n, n), f32)
    rows = lax.broadcasted_iota(jnp.int32, (nb, nb), 0)
    cols = lax.broadcasted_iota(jnp.int32, (nb, nb), 1)
    row_ids = lax.broadcasted_iota(jnp.int32, (nb, 1), 0)
    lane_ids = lax.broadcasted_iota(jnp.int32, (1, nb), 1)
    nt = (((1,), (1,)), ((), ()))
    for b in range(n // nb):
        lo, hi = b * nb, (b + 1) * nb
        d_ref[:, :nb] = a_ref[lo:hi, lo:hi]
        d_ref[:, nb:] = (rows == cols).astype(f32)

        def eliminate(t, c):
            k = 2 * t
            top = d_ref[pl.ds(k, 1), :]
            low = d_ref[pl.ds(k + 1, 1), :]
            block = d_ref[:, :nb]

            def lane(row, at):
                return jnp.sum(jnp.where(lane_ids == at, row[:, :nb], 0.0), axis=1, keepdims=True)

            def column(at):
                return jnp.sum(jnp.where(cols == at, block, 0.0), axis=1, keepdims=True)

            p11, p12, p22 = lane(top, k), lane(top, k + 1), lane(low, k + 1)
            c0, c1 = column(k), column(k + 1)
            inv1 = 1.0 / p11
            link = p12 * inv1
            inv2 = 1.0 / (p22 - p12 * link)
            low = (low - link * top) * inv2
            c1 = jnp.where(row_ids > k + 1, c1 - link * c0, 0.0)
            c0 = jnp.where(row_ids > k, c0, 0.0)
            d_ref[...] = d_ref[...] - c0 * (top * inv1) - c1 * low
            return c

        lax.fori_loop(0, nb // 2, eliminate, 0)
        pivots = jnp.sum(jnp.where(rows == cols, d_ref[:, :nb], 0.0), axis=1, keepdims=True)
        inverse = d_ref[:, nb:] / jnp.sqrt(pivots)
        w_ref[lo:hi, lo:hi] = inverse
        if lo > 0:
            mixed = jnp.dot(a_ref[lo:hi, :lo], w_ref[:lo, :lo], precision=highest, preferred_element_type=f32)
            w_ref[lo:hi, :lo] = -jnp.dot(inverse, mixed, precision=highest, preferred_element_type=f32)
        if hi < n:
            panel = lax.dot_general(a_ref[hi:, lo:hi], inverse, nt, precision=highest, preferred_element_type=f32)
            a_ref[hi:, lo:hi] = panel
            a_ref[hi:, hi:] = a_ref[hi:, hi:] - lax.dot_general(
                panel, panel, nt, precision=highest, preferred_element_type=f32
            )


def inverse_factor(blocks, n):
    nb = block_size(n)
    vmem = pl.BlockSpec(memory_space=pltpu.VMEM)
    return pl.pallas_call(
        functools.partial(factor_kernel, nb),
        out_shape=jax.ShapeDtypeStruct((n, n), f32),
        in_specs=[vmem],
        out_specs=vmem,
        scratch_shapes=[pltpu.VMEM((n, n), f32), pltpu.VMEM((nb, 2 * nb), f32)],
        compiler_params=pltpu.CompilerParams(vmem_limit_bytes=32 * 1024 * 1024),
        name="factor_inverse",
    )(blocks)


def reduce_kernel(nb, g_ref, out_ref, pack, first, part, second, full, sends, recvs_a, recvs_b, recvs_c, recvs_d):
    n = g_ref.shape[0]
    total = pack.shape[0]
    slabs, bands = lax.axis_size("slab"), lax.axis_size("band")
    my_slab, my_band = lax.axis_index("slab"), lax.axis_index("band")
    deep, thin = total // slabs, total // slabs // bands
    at = 0
    for i in range(n // nb):
        for j in range(i + 1):
            pack[at : at + nb] = g_ref[i * nb : (i + 1) * nb, j * nb : (j + 1) * nb]
            at += nb
    if at < total:
        pack[at:] = jnp.zeros((total - at, nb), f32)

    def peer(me, size, d):
        return lax.rem(me + d, size)

    barrier = pltpu.get_barrier_semaphore()
    for axis, me, size in (("slab", my_slab, slabs), ("band", my_band, bands)):
        for d in range(1, size):
            pl.semaphore_signal(
                barrier, inc=1, device_id={axis: peer(me, size, d)}, device_id_type=pl.DeviceIdType.MESH
            )
    pl.semaphore_wait(barrier, slabs + bands - 2)

    def exchange(axis, me, size, source, target, recvs):
        copies = []
        for d in range(1, size):
            other = peer(me, size, d)
            copies.append(
                pltpu.make_async_remote_copy(
                    src_ref=source(other),
                    dst_ref=target(d),
                    send_sem=sends.at[d - 1],
                    recv_sem=recvs.at[d - 1],
                    device_id={axis: other},
                    device_id_type=pl.DeviceIdType.MESH,
                )
            )
        for copy in copies:
            copy.start()
        for copy in copies:
            copy.wait()

    def span(start, length):
        return pl.ds(pl.multiple_of(start, 8), length)

    exchange(
        "slab", my_slab, slabs, lambda t: pack.at[span(t * deep, deep)], lambda d: first.at[d - 1], recvs_a
    )
    value = pack[span(my_slab * deep, deep)]
    for d in range(1, slabs):
        value = value + first[d - 1]
    part[...] = value
    exchange(
        "band", my_band, bands, lambda t: part.at[span(t * thin, thin)], lambda d: second.at[d - 1], recvs_b
    )
    value = part[span(my_band * thin, thin)]
    for d in range(1, bands):
        value = value + second[d - 1]
    mine = span(my_slab * deep + my_band * thin, thin)
    full[mine] = value
    exchange("band", my_band, bands, lambda t: full.at[mine], lambda d: full.at[mine], recvs_c)
    mine_deep = span(my_slab * deep, deep)
    exchange("slab", my_slab, slabs, lambda t: full.at[mine_deep], lambda d: full.at[mine_deep], recvs_d)
    out_ref[...] = full[...]


def block_size(n):
    return 128 if n % 128 == 0 else n


def reduced_blocks(gram):
    n = gram.shape[0]
    nb = block_size(n)
    slabs, bands = lax.axis_size("slab"), lax.axis_size("band")
    count = n // nb
    used = count * (count + 1) // 2 * nb
    unit = 8 * slabs * bands
    total = (used + unit - 1) // unit * unit
    vmem = pl.BlockSpec(memory_space=pltpu.VMEM)
    dma = pltpu.SemaphoreType.DMA
    return pl.pallas_call(
        functools.partial(reduce_kernel, nb),
        out_shape=jax.ShapeDtypeStruct((total, nb), f32),
        in_specs=[vmem],
        out_specs=vmem,
        scratch_shapes=[
            pltpu.VMEM((total, nb), f32),
            pltpu.VMEM((slabs - 1, total // slabs, nb), f32),
            pltpu.VMEM((total // slabs, nb), f32),
            pltpu.VMEM((bands - 1, total // slabs // bands, nb), f32),
            pltpu.VMEM((total, nb), f32),
            dma((max(slabs, bands) - 1,)),
            dma((slabs - 1,)),
            dma((bands - 1,)),
            dma((bands - 1,)),
            dma((slabs - 1,)),
        ],
        compiler_params=pltpu.CompilerParams(
            collective_id=1, has_side_effects=True, vmem_limit_bytes=32 * 1024 * 1024
        ),
        name="gram_sum",
    )(gram)


def local(
    orbitals, potential, projectors, atom_kind, atom_plane, atom_coef, filter_cut, filter_top
):
    rows = orbitals.shape[0]
    centre, pairs = chebyshev_scalars(filter_cut[0], filter_top[0])
    scal = []
    for a, b in pairs:
        scal += [a, jnp.zeros((), f32) if b is None else b]
    scal = jnp.stack(scal + [centre])
    filtered = filter_call(
        atom_plane, atom_kind, scal, orbitals, potential, atom_coef, projectors, 2 if rows % 32 == 0 else 1
    )
    grid_layout = filtered.reshape(-1, filtered.shape[2])
    point_total = grid_layout.shape[1] * lax.axis_size(("band", "slab"))
    gram = jnp.dot(grid_layout, grid_layout.T, precision=highest) / point_total
    factor_inverse = inverse_factor(reduced_blocks(gram), gram.shape[0])
    return jnp.dot(factor_inverse, grid_layout, precision=lax.Precision.HIGH)


def solution(mesh):
    in_specs = (
        P("band", "slab", None),
        P("slab", None),
        P(),
        P("slab"),
        P("slab"),
        P("slab", None),
        P(),
        P(),
    )
    out_specs = P(None, ("slab", "band"))
    return jax.shard_map(local, mesh=mesh, in_specs=in_specs, out_specs=out_specs, check_vma=False)
```

time: 203 us -> 173 us (0.85)
  blocking collectives: 53.7 us -> 0 us
  Pallas kernels: 132 us -> 161 us
  local copies, waits for them, and re-layouts: 6.21 us -> 0.64 us
  other arithmetic: 2.25 us -> 0 us
  matrix products: 6.69 us -> 8.91 us
    all_to_all x1 -> x0, blocking collectives: 53.7 us -> none  [local(): lax.all_to_all(filtered, 'band', split_axis=0, concat_axis=0, tiled=True)]
    pallas_call x1, Pallas kernels: 67.7 us -> 93.5 us  [filter_call(): pl.pallas_call(functools.partial(filter_kernel, groups), out_shape=jax.Sh...]
    unnamed x3 -> x2, local copies, waits for them, and re-layouts: 4.14 us -> 0.01 us
    pallas_call x1, Pallas kernels: 28.8 us -> 32.2 us  [reduced_blocks(): pl.pallas_call(functools.partial(reduce_kernel, nb), out_shape=jax.ShapeD...]
    dot_general x1, matrix products: 3.52 us -> 5.74 us  [local(): gram = jnp.dot(grid_layout, grid_layout.T, precision=highest) / point_total]
where the time goes in v1:
time: 173 us
  Pallas kernels  161 us (93%)
  matrix products  8.91 us (5%)
  between operations  1.88 us (1%)
    pallas_call x1, Pallas kernels, filter_call(): pl.pallas_call(functools.partial(filter_kernel, groups), out_shape=jax.Sh...  93.5 us
    pallas_call x1, Pallas kernels, inverse_factor(): pl.pallas_call(functools.partial(factor_kernel, nb), out_shape=jax.ShapeD...  35.6 us
    pallas_call x1, Pallas kernels, reduced_blocks(): pl.pallas_call(functools.partial(reduce_kernel, nb), out_shape=jax.ShapeD...  32.2 us
    dot_general x1, matrix products, local(): gram = jnp.dot(grid_layout, grid_layout.T, precision=highest) / point_total  5.74 us

profile of v1, /device:TPU:1, one launch (start us, length us, event | category | flops | bytes accessed | tf_op | source)
XLA Modules:
  0.0 172.8 jit_solution(10758766926104482217)
XLA Ops:
  1.8 0.6 stack.48.scal_ref
  2.5 93.5 %cheb_filter.1 = f32[8,64,1024]{2,1,0:T(8,128)} custom-call(s32[8]{0:T(128)} %plane_ref.1, s32[8]{0:T(128)} %kind_ref.1, f32[13]{0:T(128)} %stack.48.scal_ref, f32[64,16,512]{2,1,0:T(8,128)} %orb_ref.1, f32[16,512]{1,0:T(8,128)} %pot_ref.1, f32[8,128]{1,0:T(8,128)} %coef_ref.1, f32[4,2048,128]{2,1,0:T(8,128)} %proj_ref.1), custom_call_target="tpu_custom_call" | custom-call | tf_op jit(solution)/shard_map/cheb_filter/pallas_call | solution.py:274
  96.0 5.7 %convolution_multiply_fusion.g_ref = f32[512,512]{1,0:T(8,128)S(1)} fusion(f32[512,1024]{1,0:T(8,128)} %bitcast.18), kind=kOutput, calls=%fused_computation | convolution fusion | flops 3221487616 | bytes 3145728 | tf_op jit(solution)/shard_map/dot_general | solution.py:495
  101.7 0.0 copy-start
  101.7 32.2 %gram_sum.1.g_ref = f32[1280,128]{1,0:T(8,128)S(1)} custom-call(f32[512,512]{1,0:T(8,128)S(1)} %convolution_multiply_fusion.g_ref), custom_call_target="tpu_custom_call" | custom-call | tf_op jit(solution)/shard_map/gram_sum/pallas_call | solution.py:457
  134.0 35.6 %factor_inverse.1 = f32[512,512]{1,0:T(8,128)S(1)} custom-call(f32[1280,128]{1,0:T(8,128)S(1)} %gram_sum.1.g_ref), custom_call_target="tpu_custom_call" | custom-call | tf_op jit(solution)/shard_map/factor_inverse/pallas_call | solution.py:364
  169.6 0.0 copy-done
  169.6 3.2 %fusion = f32[512,1024]{1,0:T(8,128)} fusion(f32[512,512]{1,0:T(8,128)S(1)} %factor_inverse.1, f32[512,1024]{1,0:T(8,128)S(1)} %bitcast.19), kind=kOutput, calls=%fused_computation.1 | convolution fusion | flops 1610612736 | bytes 5242880 | tf_op jit(solution)/shard_map/dot_general | solution.py:497
Async XLA Ops:
  101.7 67.9 %copy-start = (f32[8,64,1024]{2,1,0:T(8,128)S(1)}, f32[8,64,1024]{2,1,0:T(8,128)}, u32[]{:S(2)}) copy-start(f32[8,64,1024]{2,1,0:T(8,128)} %cheb_filter.1) | copy-start | bytes 6291460

commit v2 on v1

--- a/solution.py
+++ b/solution.py
@@ -34,9 +34,13 @@
     return centre, pairs
 
 
+def pair_slots(atoms, kinds):
+    return min(atoms, (atoms + kinds) // 2)
+
+
 def filter_kernel(
     groups, plane_ref, kind_ref, scal_ref, orb_ref, pot_ref, coef_ref, proj_ref,
-    out_ref, table, back, lap, even, odd, split, spread, halo, raw, load_sem, table_sem, own_sem,
+    out_ref, table, back, lap, even, odd, split, spread, halo, raw, pairs, load_sem, table_sem, own_sem,
     send_sem, recv_sem, out_sem, in_sem,
 ):
     rows, planes, points = orb_ref.shape
@@ -78,7 +82,7 @@
         spread[a, depth + 1] = zeros[:share]
         return c
 
-    lax.fori_loop(0, atoms, clear_spread, 0)
+    lax.fori_loop(0, spread.shape[0], clear_spread, 0)
 
     strip = 64
 
@@ -115,6 +119,45 @@
 
     for copy in loads:
         copy.wait()
+
+    slot_count = pair_slots(atoms, kinds)
+    kind_of = [jnp.clip(kind_ref[a], 0, kinds - 1) for a in range(atoms)]
+    base, bases = 0, []
+    for k in range(kinds):
+        bases.append(base)
+        base = base + (sum((kind_of[a] == k).astype(jnp.int32) for a in range(atoms)) + 1) // 2
+    seats = []
+    for a in range(atoms):
+        rank = sum(((kind_of[b] == kind_of[a]).astype(jnp.int32) for b in range(a)), jnp.int32(0))
+        start = sum(jnp.where(kind_of[a] == k, bases[k], 0) for k in range(kinds))
+        seats.append(2 * start + rank)
+        pairs[0, a] = seats[a]
+    for seat in range(2 * slot_count):
+        holder = sum(jnp.where(seats[a] == seat, a + 1, 0) for a in range(atoms))
+        pairs[1, seat] = holder
+    zero_row = jnp.zeros((1, funcs), f32)
+    half = 16 if share % 16 == 0 else share
+
+    def copies_from(source, g, s, piece):
+        found = []
+        for h in range(share // half) if piece is None else (piece,):
+            rs = pl.ds(pl.multiple_of(g * share + h * half, 8), half)
+            for side, start, target in ((0, planes - 2, right), (1, 0, left)):
+                found.append(
+                    pltpu.make_async_remote_copy(
+                        src_ref=source.at[pl.ds(start, 2), rs],
+                        dst_ref=halo.at[g, s, side, h],
+                        send_sem=send_sem.at[g, side, h],
+                        recv_sem=recv_sem.at[g, s, side, h],
+                        device_id={"slab": target},
+                        device_id_type=MESH,
+                    )
+                )
+        return found
+
+    for g in range(groups):
+        for copy in copies_from(even, g, 0, None):
+            copy.start()
 
     centre = scal_ref[2 * ORDER]
     quad = 4
@@ -162,45 +205,46 @@
         def step(s, cur, nxt):
             scale = scal_ref[2 * s]
             pull = scal_ref[2 * s + 1]
-            copies = []
-            for side, start, target in ((0, planes - 2, right), (1, 0, left)):
-                copy = pltpu.make_async_remote_copy(
-                    src_ref=cur.at[pl.ds(start, 2), rs],
-                    dst_ref=halo.at[g, s, side],
-                    send_sem=send_sem.at[side],
-                    recv_sem=recv_sem.at[g, s, side],
-                    device_id={"slab": target},
-                    device_id_type=MESH,
+            def pair(q, c):
+                holders = [pairs[1, 2 * q + m] for m in range(2)]
+                atom = [jnp.maximum(holder - 1, 0) for holder in holders]
+                k = jnp.clip(kind_ref[atom[0]], 0, kinds - 1)
+                places = [jnp.clip(plane_ref[atom[m]] - me * planes, 0, planes - depth) for m in range(2)]
+                both = jnp.concatenate(
+                    [jnp.concatenate([split[p + j] for j in range(depth)], axis=1) for p in places], axis=0
                 )
-                copy.start()
-                copies.append(copy)
-
-            def atom(a, c):
-                p = jnp.clip(plane_ref[a] - me * planes, 0, planes - depth)
-                k = kind_ref[a]
-                both = jnp.concatenate([split[p + j] for j in range(depth)], axis=1)
                 r = jnp.dot(both, table[k], preferred_element_type=f32)
-                coupled = r[:share, :funcs] + (r[:share, funcs:] + r[share:, :funcs])
-                high, low = halves(coupled * coef_ref[pl.ds(a, 1)])
-                pair = jnp.concatenate(
-                    [jnp.concatenate([high, high], axis=1), jnp.concatenate([low, low], axis=1)], axis=0
-                )
+                stack = []
+                for m in range(2):
+                    at = m * 2 * share
+                    coupled = r[at : at + share, :funcs] + (
+                        r[at : at + share, funcs:] + r[at + share : at + 2 * share, :funcs]
+                    )
+                    coef = jnp.where(holders[m] > 0, coef_ref[pl.ds(atom[m], 1)], zero_row)
+                    for value in halves(coupled * coef):
+                        stack.append(jnp.concatenate([value, value], axis=1))
+                stack = jnp.concatenate(stack, axis=0)
                 for j in range(depth):
-                    r = jnp.dot(pair, back[k, :, j * points : (j + 1) * points], preferred_element_type=f32)
-                    spread[a, j + 1] = r[:share] + r[share:]
+                    r = jnp.dot(stack, back[k, :, j * points : (j + 1) * points], preferred_element_type=f32)
+                    for m in range(2):
+                        at = m * 2 * share
+                        spread[2 * q + m, j + 1] = r[at : at + share] + r[at + share : at + 2 * share]
                 return c
 
-            lax.fori_loop(0, atoms, atom, 0, unroll=True)
-
+            lax.fori_loop(0, slot_count, pair, 0, unroll=True)
+
+            seat_of = [pairs[0, a] for a in range(atoms)]
             slots = {x: [jnp.clip(x - places[a], -1, depth) + 1 for a in range(atoms)] for x in range(planes)}
 
-            def quads(xs, take):
+            def quads(xs, take, before=None, after=None):
                 both = jnp.concatenate([split[x] for x in xs], axis=0)
                 r = jnp.dot(both, lap[...], preferred_element_type=f32)
                 piece = min(16, share)
                 span = min(256, points)
                 for r0, l0 in [(r0, l0) for r0 in range(0, share, piece) for l0 in range(0, points, span)]:
                     ls = slice(l0, l0 + span)
+                    if before is not None and r0 % half == 0 and l0 == 0:
+                        before(r0 // half)
                     fs = {}
                     for x in xs:
                         for d in (-2, -1, 0, 1, 2):
@@ -212,26 +256,37 @@
                         total = total + (pot_ref[pl.ds(x, 1), ls] + (1.25 - centre)) * fs[x]
                         total = total + (fs[x - 1] + fs[x + 1]) * (-2.0 / 3.0) + (fs[x - 2] + fs[x + 2]) * (1.0 / 24.0)
                         for a in range(atoms):
-                            total = total + spread[a, slots[x][a], r0 : r0 + piece, ls]
+                            total = total + spread[seat_of[a], slots[x][a], r0 : r0 + piece, ls]
                         at = (x, pl.ds(first + r0, piece), ls)
                         fresh = scale * total - pull * nxt[at]
                         nxt[at] = fresh
                         high, low = halves(fresh)
                         split[x, r0 : r0 + piece, ls] = high
                         split[x, share + r0 : share + r0 + piece, ls] = low
+                    if after is not None and (r0 + piece) % half == 0 and l0 + span == points:
+                        after(r0 // half)
 
             def take(x, r0, piece, ls):
                 if x < 0:
-                    return halo[g, s, 0, x + 2, r0 : r0 + piece, ls]
+                    return halo[g, s, 0, r0 // half, x + 2, r0 % half : r0 % half + piece, ls]
                 if x >= planes:
-                    return halo[g, s, 1, x - planes, r0 : r0 + piece, ls]
+                    return halo[g, s, 1, r0 // half, x - planes, r0 % half : r0 % half + piece, ls]
                 return cur[x, pl.ds(first + r0, piece), ls]
 
             for x0 in range(2, planes - 2, quad):
                 quads(list(range(x0, min(x0 + quad, planes - 2))), take)
-            for copy in copies:
-                copy.wait()
-            quads([0, 1, planes - 2, planes - 1], take)
+
+            def before(h):
+                for copy in copies_from(cur, g, s, h):
+                    copy.wait()
+
+            def after(h):
+                @pl.when(s + 1 < ORDER)
+                def _():
+                    for copy in copies_from(nxt, g, s + 1, h):
+                        copy.start()
+
+            quads([0, 1, planes - 2, planes - 1], take, before, after)
 
         def two(i, c):
             step(2 * i, even, odd)
@@ -267,6 +322,7 @@
     share = rows // groups
     width = planes * points // bands
     units = max(width // points, 1)
+    half = 16 if share % 16 == 0 else share
     smem = pl.BlockSpec(memory_space=pltpu.SMEM)
     vmem = pl.BlockSpec(memory_space=pltpu.VMEM)
     hbm = pl.BlockSpec(memory_space=pl.ANY)
@@ -283,14 +339,15 @@
             pltpu.VMEM((planes, rows, points), f32),
             pltpu.VMEM((planes, rows, points), f32),
             pltpu.VMEM((planes, 2 * share, points), bf16),
-            pltpu.VMEM((atoms, depth + 2, share, points), f32),
-            pltpu.VMEM((groups, ORDER, 2, 2, share, points), f32),
+            pltpu.VMEM((2 * pair_slots(atoms, kinds), depth + 2, share, points), f32),
+            pltpu.VMEM((groups, ORDER, 2, share // half, 2, half, points), f32),
             pltpu.VMEM((kinds, block, funcs), f32),
+            pltpu.SMEM((2, max(atoms, 2 * pair_slots(atoms, kinds))), jnp.int32),
             dma((planes,)),
             dma((kinds,)),
             dma((units,)),
-            dma((2,)),
-            dma((groups, ORDER, 2)),
+            dma((groups, 2, share // half)),
+            dma((groups, ORDER, 2, share // half)),
             dma((groups, bands - 1, units)),
             dma((groups, bands - 1, units)),
         ],

time: 173 us -> 163 us (0.942)
  Pallas kernels: 161 us -> 152 us
    pallas_call x1, Pallas kernels: 93.5 us -> 83.5 us  [filter_call(): pl.pallas_call(functools.partial(filter_kernel, groups), out_shape=jax.Sh...]
where the time goes in v2:
time: 163 us
  Pallas kernels  152 us (93%)
  matrix products  8.91 us (5%)
  between operations  1.88 us (1%)
    pallas_call x1, Pallas kernels, filter_call(): pl.pallas_call(functools.partial(filter_kernel, groups), out_shape=jax.Sh...  83.5 us
    pallas_call x1, Pallas kernels, inverse_factor(): pl.pallas_call(functools.partial(factor_kernel, nb), out_shape=jax.ShapeD...  35.6 us
    pallas_call x1, Pallas kernels, reduced_blocks(): pl.pallas_call(functools.partial(reduce_kernel, nb), out_shape=jax.ShapeD...  32.4 us
    dot_general x1, matrix products, local(): gram = jnp.dot(grid_layout, grid_layout.T, precision=highest) / point_total  5.74 us

profile of v2, /device:TPU:1, one launch (start us, length us, event | category | flops | bytes accessed | tf_op | source)
XLA Modules:
  0.0 162.9 jit_solution(9961965326836319899)
XLA Ops:
  1.8 0.6 stack.48.scal_ref
  2.5 83.5 %cheb_filter.1 = f32[8,64,1024]{2,1,0:T(8,128)} custom-call(s32[8]{0:T(128)} %plane_ref.1, s32[8]{0:T(128)} %kind_ref.1, f32[13]{0:T(128)} %stack.48.scal_ref, f32[64,16,512]{2,1,0:T(8,128)} %orb_ref.1, f32[16,512]{1,0:T(8,128)} %pot_ref.1, f32[8,128]{1,0:T(8,128)} %coef_ref.1, f32[4,2048,128]{2,1,0:T(8,128)} %proj_ref.1), custom_call_target="tpu_custom_call" | custom-call | tf_op jit(solution)/shard_map/cheb_filter/pallas_call | solution.py:330
  86.0 5.7 %convolution_multiply_fusion.g_ref = f32[512,512]{1,0:T(8,128)S(1)} fusion(f32[512,1024]{1,0:T(8,128)} %bitcast.18), kind=kOutput, calls=%fused_computation | convolution fusion | flops 3221487616 | bytes 3145728 | tf_op jit(solution)/shard_map/dot_general | solution.py:552
  91.7 0.0 copy-start
  91.7 32.4 %gram_sum.1.g_ref = f32[1280,128]{1,0:T(8,128)S(1)} custom-call(f32[512,512]{1,0:T(8,128)S(1)} %convolution_multiply_fusion.g_ref), custom_call_target="tpu_custom_call" | custom-call | tf_op jit(solution)/shard_map/gram_sum/pallas_call | solution.py:514
  124.2 35.6 %factor_inverse.1 = f32[512,512]{1,0:T(8,128)S(1)} custom-call(f32[1280,128]{1,0:T(8,128)S(1)} %gram_sum.1.g_ref), custom_call_target="tpu_custom_call" | custom-call | tf_op jit(solution)/shard_map/factor_inverse/pallas_call | solution.py:421
  159.8 0.0 copy-done
  159.8 3.2 %fusion = f32[512,1024]{1,0:T(8,128)} fusion(f32[512,512]{1,0:T(8,128)S(1)} %factor_inverse.1, f32[512,1024]{1,0:T(8,128)S(1)} %bitcast.19), kind=kOutput, calls=%fused_computation.1 | convolution fusion | flops 1610612736 | bytes 5242880 | tf_op jit(solution)/shard_map/dot_general | solution.py:554
Async XLA Ops:
  91.7 68.0 %copy-start = (f32[8,64,1024]{2,1,0:T(8,128)S(1)}, f32[8,64,1024]{2,1,0:T(8,128)}, u32[]{:S(2)}) copy-start(f32[8,64,1024]{2,1,0:T(8,128)} %cheb_filter.1) | copy-start | bytes 6291460

commit v3 on v2

--- a/solution.py
+++ b/solution.py
@@ -8,6 +8,7 @@
 
 GZ = 32
 ORDER = 6
+micro = 8
 
 low_edge = -1.0
 highest = lax.Precision.HIGHEST
@@ -358,181 +359,233 @@
     )(plane, kind, scal, orb, pot, coef, proj)
 
 
-def factor_kernel(nb, g_ref, w_ref, a_ref, d_ref):
+def invert_block(t_ref, cols_ref, nb):
+    lanes = lax.broadcasted_iota(jnp.int32, (micro, nb), 1)
+    subs = lax.broadcasted_iota(jnp.int32, (micro, nb), 0)
+    for k in range(0, nb, micro):
+        inside = (lanes >= k) & (lanes < k + micro)
+        head = t_ref[k : k + micro, :]
+        for t in range(micro):
+            cols_ref[t] = jnp.broadcast_to(head[:, k + t : k + t + 1], (micro, nb))
+        rows = [
+            jnp.where(inside, (lanes == k + t).astype(f32), jnp.broadcast_to(t_ref[k + t : k + t + 1, :], (micro, nb)))
+            for t in range(micro)
+        ]
+        e = {
+            (s, t): jnp.broadcast_to(cols_ref[t, s : s + 1, :], (micro, nb))
+            for t in range(micro)
+            for s in range(t, micro)
+        }
+        link, inv = {}, []
+        for t in range(micro):
+            inv.append(1.0 / e[t, t])
+            for s in range(t + 1, micro):
+                link[s, t] = e[s, t] * inv[t]
+            for s in range(t + 1, micro):
+                for u in range(t + 1, s + 1):
+                    e[s, u] = e[s, u] - link[s, t] * e[u, t]
+                rows[s] = rows[s] - link[s, t] * rows[t]
+        solved = [rows[t] * inv[t] for t in range(micro)]
+        for s in range(micro - 1, 0, -1):
+            for t in range(s):
+                solved[t] = solved[t] - link[s, t] * solved[s]
+        for i in range(k + micro, nb, micro):
+            tile = t_ref[i : i + micro, :]
+            parts = [jnp.broadcast_to(tile[:, k + t : k + t + 1], (micro, nb)) * solved[t] for t in range(micro)]
+            while len(parts) > 1:
+                parts = [parts[j] + parts[j + 1] for j in range(0, len(parts), 2)]
+            t_ref[i : i + micro, :] = jnp.where(inside, 0.0, tile) - parts[0]
+        final = jnp.zeros((micro, nb), f32)
+        for t in range(micro):
+            final = jnp.where(subs == t, rows[t] * lax.rsqrt(e[t, t]), final)
+        t_ref[k : k + micro, :] = jnp.where(lanes < k + micro, final, 0.0)
+
+
+def factor_body(nb, a_ref, w_ref, t_ref, cols_ref):
     n = w_ref.shape[0]
-    a_ref[...] = jnp.zeros((n, n), f32)
-    at = 0
-    for i in range(n // nb):
-        for j in range(i + 1):
-            a_ref[i * nb : (i + 1) * nb, j * nb : (j + 1) * nb] = g_ref[at : at + nb]
-            at += nb
-    w_ref[...] = jnp.zeros((n, n), f32)
-    rows = lax.broadcasted_iota(jnp.int32, (nb, nb), 0)
-    cols = lax.broadcasted_iota(jnp.int32, (nb, nb), 1)
-    row_ids = lax.broadcasted_iota(jnp.int32, (nb, 1), 0)
-    lane_ids = lax.broadcasted_iota(jnp.int32, (1, nb), 1)
     nt = (((1,), (1,)), ((), ()))
-    for b in range(n // nb):
-        lo, hi = b * nb, (b + 1) * nb
-        d_ref[:, :nb] = a_ref[lo:hi, lo:hi]
-        d_ref[:, nb:] = (rows == cols).astype(f32)
-
-        def eliminate(t, c):
-            k = 2 * t
-            top = d_ref[pl.ds(k, 1), :]
-            low = d_ref[pl.ds(k + 1, 1), :]
-            block = d_ref[:, :nb]
-
-            def lane(row, at):
-                return jnp.sum(jnp.where(lane_ids == at, row[:, :nb], 0.0), axis=1, keepdims=True)
-
-            def column(at):
-                return jnp.sum(jnp.where(cols == at, block, 0.0), axis=1, keepdims=True)
-
-            p11, p12, p22 = lane(top, k), lane(top, k + 1), lane(low, k + 1)
-            c0, c1 = column(k), column(k + 1)
-            inv1 = 1.0 / p11
-            link = p12 * inv1
-            inv2 = 1.0 / (p22 - p12 * link)
-            low = (low - link * top) * inv2
-            c1 = jnp.where(row_ids > k + 1, c1 - link * c0, 0.0)
-            c0 = jnp.where(row_ids > k, c0, 0.0)
-            d_ref[...] = d_ref[...] - c0 * (top * inv1) - c1 * low
-            return c
-
-        lax.fori_loop(0, nb // 2, eliminate, 0)
-        pivots = jnp.sum(jnp.where(rows == cols, d_ref[:, :nb], 0.0), axis=1, keepdims=True)
-        inverse = d_ref[:, nb:] / jnp.sqrt(pivots)
-        w_ref[lo:hi, lo:hi] = inverse
-        if lo > 0:
-            mixed = jnp.dot(a_ref[lo:hi, :lo], w_ref[:lo, :lo], precision=highest, preferred_element_type=f32)
-            w_ref[lo:hi, :lo] = -jnp.dot(inverse, mixed, precision=highest, preferred_element_type=f32)
-        if hi < n:
-            panel = lax.dot_general(a_ref[hi:, lo:hi], inverse, nt, precision=highest, preferred_element_type=f32)
-            a_ref[hi:, lo:hi] = panel
-            a_ref[hi:, hi:] = a_ref[hi:, hi:] - lax.dot_general(
-                panel, panel, nt, precision=highest, preferred_element_type=f32
-            )
-
-
-def inverse_factor(blocks, n):
-    nb = block_size(n)
-    vmem = pl.BlockSpec(memory_space=pltpu.VMEM)
-    return pl.pallas_call(
-        functools.partial(factor_kernel, nb),
-        out_shape=jax.ShapeDtypeStruct((n, n), f32),
-        in_specs=[vmem],
-        out_specs=vmem,
-        scratch_shapes=[pltpu.VMEM((n, n), f32), pltpu.VMEM((nb, 2 * nb), f32)],
-        compiler_params=pltpu.CompilerParams(vmem_limit_bytes=32 * 1024 * 1024),
-        name="factor_inverse",
-    )(blocks)
-
-
-def reduce_kernel(nb, g_ref, out_ref, pack, first, part, second, full, sends, recvs_a, recvs_b, recvs_c, recvs_d):
-    n = g_ref.shape[0]
+    count = n // nb
+
+    def one(b, c):
+        at = pl.ds(pl.multiple_of(b * nb, nb), nb)
+        t_ref[...] = a_ref[at, at]
+        invert_block(t_ref, cols_ref, nb)
+        for i in range(count):
+
+            @pl.when(b == i)
+            def _():
+                lo, hi = i * nb, (i + 1) * nb
+                inverse = t_ref[...]
+                w_ref[lo:hi, lo:hi] = inverse
+                if hi < n:
+                    w_ref[lo:hi, hi:] = jnp.zeros((nb, n - hi), f32)
+                    panel = lax.dot_general(a_ref[hi:, lo:hi], inverse, nt, precision=highest, preferred_element_type=f32)
+                    a_ref[hi:, lo:hi] = panel
+                    a_ref[hi:, hi:] = a_ref[hi:, hi:] - lax.dot_general(
+                        panel, panel, nt, precision=highest, preferred_element_type=f32
+                    )
+                if lo > 0:
+                    mixed = jnp.dot(a_ref[lo:hi, :lo], w_ref[:lo, :lo], precision=highest, preferred_element_type=f32)
+                    w_ref[lo:hi, :lo] = -jnp.dot(inverse, mixed, precision=highest, preferred_element_type=f32)
+
+        return c
+
+    lax.fori_loop(0, count, one, 0)
+
+
+def orthogonal_kernel(
+    nb, point_total, f_ref, w_ref, stack, pack, first, part, second, full, a_ref, t_ref, cols_ref,
+    pair_sems, sum_send, sum_recv, gather_send, gather_recv, relay_send, relay_recv,
+):
+    n = w_ref.shape[0]
+    count = n // nb
     total = pack.shape[0]
     slabs, bands = lax.axis_size("slab"), lax.axis_size("band")
     my_slab, my_band = lax.axis_index("slab"), lax.axis_index("band")
-    deep, thin = total // slabs, total // slabs // bands
+    lines = slabs // 2
+    chips = bands * lines
+    core, chip = lax.rem(my_slab, 2), my_band * lines + my_slab // 2
+    partner = my_slab + 1 - 2 * core
+    deep = total // 2
+    thin = deep // chips
+    base = core * deep
+
+    barrier = pltpu.get_barrier_semaphore()
+
+    def place(d):
+        other = lax.rem(chip + d, chips)
+        return other, {"band": other // lines, "slab": lax.rem(other, lines) * 2 + core}
+
+    def greet(d, c):
+        pl.semaphore_signal(barrier, inc=1, device_id=place(d)[1], device_id_type=MESH)
+        return c
+
+    pl.semaphore_signal(barrier, inc=1, device_id={"slab": partner}, device_id_type=MESH)
+    lax.fori_loop(1, chips, greet, 0)
+
+    for i in range(count):
+        rows = pl.ds(i * nb, nb)
+        high, low = halves(f_ref[rows, :])
+        stack[i, :nb] = high
+        stack[i, nb:] = low
     at = 0
-    for i in range(n // nb):
-        for j in range(i + 1):
-            pack[at : at + nb] = g_ref[i * nb : (i + 1) * nb, j * nb : (j + 1) * nb]
+    for j in range(count):
+        for i in range(j, count):
+            r = lax.dot_general(stack[i], stack[j], (((1,), (1,)), ((), ())), preferred_element_type=f32)
+            r = (r[:nb, :nb] + r[nb:, nb:]) + (r[:nb, nb:] + r[nb:, :nb])
+            pack[at : at + nb] = r * (1.0 / point_total)
             at += nb
     if at < total:
         pack[at:] = jnp.zeros((total - at, nb), f32)
 
-    def peer(me, size, d):
-        return lax.rem(me + d, size)
-
-    barrier = pltpu.get_barrier_semaphore()
-    for axis, me, size in (("slab", my_slab, slabs), ("band", my_band, bands)):
-        for d in range(1, size):
-            pl.semaphore_signal(
-                barrier, inc=1, device_id={axis: peer(me, size, d)}, device_id_type=pl.DeviceIdType.MESH
-            )
-    pl.semaphore_wait(barrier, slabs + bands - 2)
-
-    def exchange(axis, me, size, source, target, recvs):
-        copies = []
-        for d in range(1, size):
-            other = peer(me, size, d)
-            copies.append(
-                pltpu.make_async_remote_copy(
-                    src_ref=source(other),
-                    dst_ref=target(d),
-                    send_sem=sends.at[d - 1],
-                    recv_sem=recvs.at[d - 1],
-                    device_id={axis: other},
-                    device_id_type=pl.DeviceIdType.MESH,
-                )
-            )
-        for copy in copies:
-            copy.start()
-        for copy in copies:
-            copy.wait()
+    pl.semaphore_wait(barrier, chips)
 
     def span(start, length):
         return pl.ds(pl.multiple_of(start, 8), length)
 
-    exchange(
-        "slab", my_slab, slabs, lambda t: pack.at[span(t * deep, deep)], lambda d: first.at[d - 1], recvs_a
+    swap = pltpu.make_async_remote_copy(
+        src_ref=pack.at[span((1 - core) * deep, deep)], dst_ref=first, send_sem=pair_sems.at[0],
+        recv_sem=pair_sems.at[1], device_id={"slab": partner}, device_id_type=MESH,
     )
-    value = pack[span(my_slab * deep, deep)]
-    for d in range(1, slabs):
-        value = value + first[d - 1]
-    part[...] = value
-    exchange(
-        "band", my_band, bands, lambda t: part.at[span(t * thin, thin)], lambda d: second.at[d - 1], recvs_b
-    )
-    value = part[span(my_band * thin, thin)]
-    for d in range(1, bands):
-        value = value + second[d - 1]
-    mine = span(my_slab * deep + my_band * thin, thin)
-    full[mine] = value
-    exchange("band", my_band, bands, lambda t: full.at[mine], lambda d: full.at[mine], recvs_c)
-    mine_deep = span(my_slab * deep, deep)
-    exchange("slab", my_slab, slabs, lambda t: full.at[mine_deep], lambda d: full.at[mine_deep], recvs_d)
-    out_ref[...] = full[...]
-
-
-def block_size(n):
-    return 128 if n % 128 == 0 else n
-
-
-def reduced_blocks(gram):
-    n = gram.shape[0]
-    nb = block_size(n)
+    swap.start()
+    swap.wait()
+    part[...] = pack[span(base, deep)] + first[...]
+
+    def scatter(d):
+        other, device = place(d)
+        return pltpu.make_async_remote_copy(
+            src_ref=part.at[span(other * thin, thin)], dst_ref=second.at[d - 1], send_sem=sum_send.at[d - 1],
+            recv_sem=sum_recv.at[d - 1], device_id=device, device_id_type=MESH,
+        )
+
+    def mine(c):
+        return span(base + c * thin, thin)
+
+    def gather(d):
+        return pltpu.make_async_remote_copy(
+            src_ref=full.at[mine(chip)], dst_ref=full.at[mine(chip)], send_sem=gather_send.at[d - 1],
+            recv_sem=gather_recv.at[d - 1], device_id=place(d)[1], device_id_type=MESH,
+        )
+
+    def relay(d):
+        rows = mine(lax.rem(chip + chips - d, chips))
+        return pltpu.make_async_remote_copy(
+            src_ref=full.at[rows], dst_ref=full.at[rows], send_sem=relay_send.at[d], recv_sem=relay_recv.at[d],
+            device_id={"slab": partner}, device_id_type=MESH,
+        )
+
+    def each(first_index, action):
+        def body(d, c):
+            action(d)
+            return c
+
+        lax.fori_loop(first_index, chips, body, 0)
+
+    each(1, lambda d: scatter(d).start())
+    each(1, lambda d: scatter(d).wait())
+
+    def accumulate(d, value):
+        return value + second[d - 1]
+
+    full[mine(chip)] = lax.fori_loop(1, chips, accumulate, part[span(chip * thin, thin)])
+    each(1, lambda d: gather(d).start())
+    relay(0).start()
+
+    def pass_on(d):
+        gather(d).wait()
+        relay(d).start()
+
+    each(1, pass_on)
+    each(0, lambda d: relay(d).wait())
+
+    a_ref[...] = jnp.zeros((n, n), f32)
+    at = 0
+    for j in range(count):
+        for i in range(j, count):
+            a_ref[i * nb : (i + 1) * nb, j * nb : (j + 1) * nb] = full[at : at + nb]
+            at += nb
+    factor_body(nb, a_ref, w_ref, t_ref, cols_ref)
+
+
+def inverse_factor(grid_layout):
+    n, width = grid_layout.shape
+    nb = 128 if n % 128 == 0 else n
     slabs, bands = lax.axis_size("slab"), lax.axis_size("band")
+    chips = bands * slabs // 2
     count = n // nb
     used = count * (count + 1) // 2 * nb
-    unit = 8 * slabs * bands
+    unit = 16 * chips
     total = (used + unit - 1) // unit * unit
     vmem = pl.BlockSpec(memory_space=pltpu.VMEM)
     dma = pltpu.SemaphoreType.DMA
     return pl.pallas_call(
-        functools.partial(reduce_kernel, nb),
-        out_shape=jax.ShapeDtypeStruct((total, nb), f32),
+        functools.partial(orthogonal_kernel, nb, width * slabs * bands),
+        out_shape=jax.ShapeDtypeStruct((n, n), f32),
         in_specs=[vmem],
         out_specs=vmem,
         scratch_shapes=[
+            pltpu.VMEM((count, 2 * nb, width), bf16),
             pltpu.VMEM((total, nb), f32),
-            pltpu.VMEM((slabs - 1, total // slabs, nb), f32),
-            pltpu.VMEM((total // slabs, nb), f32),
-            pltpu.VMEM((bands - 1, total // slabs // bands, nb), f32),
+            pltpu.VMEM((total // 2, nb), f32),
+            pltpu.VMEM((total // 2, nb), f32),
+            pltpu.VMEM((chips - 1, total // 2 // chips, nb), f32),
             pltpu.VMEM((total, nb), f32),
-            dma((max(slabs, bands) - 1,)),
-            dma((slabs - 1,)),
-            dma((bands - 1,)),
-            dma((bands - 1,)),
-            dma((slabs - 1,)),
+            pltpu.VMEM((n, n), f32),
+            pltpu.VMEM((nb, nb), f32),
+            pltpu.VMEM((micro, micro, nb), f32),
+            dma((2,)),
+            dma((chips - 1,)),
+            dma((chips - 1,)),
+            dma((chips - 1,)),
+            dma((chips - 1,)),
+            dma((chips,)),
+            dma((chips,)),
         ],
         compiler_params=pltpu.CompilerParams(
             collective_id=1, has_side_effects=True, vmem_limit_bytes=32 * 1024 * 1024
         ),
-        name="gram_sum",
-    )(gram)
+        name="gram_factor",
+    )(grid_layout)
 
 
 def local(
@@ -548,9 +601,7 @@
         atom_plane, atom_kind, scal, orbitals, potential, atom_coef, projectors, 2 if rows % 32 == 0 else 1
     )
     grid_layout = filtered.reshape(-1, filtered.shape[2])
-    point_total = grid_layout.shape[1] * lax.axis_size(("band", "slab"))
-    gram = jnp.dot(grid_layout, grid_layout.T, precision=highest) / point_total
-    factor_inverse = inverse_factor(reduced_blocks(gram), gram.shape[0])
+    factor_inverse = inverse_factor(grid_layout)
     return jnp.dot(factor_inverse, grid_layout, precision=lax.Precision.HIGH)
 
 

time: 163 us -> 138 us (0.85); the launches traced: 163 us -> 136 us
  Pallas kernels: 152 us -> 129 us
  matrix products: 8.91 us -> 3.17 us
    pallas_call x2 -> x1, Pallas kernels: 68 us -> 45.4 us  [inverse_factor(): pl.pallas_call(functools.partial(orthogonal_kernel, nb, width * slabs * b...]
    dot_general x1 -> x0, matrix products: 5.74 us -> none  [local(): gram = jnp.dot(grid_layout, grid_layout.T, precision=highest) / point_total]
where the time goes in v3:
time: 138 us; the launch traced here: 136 us
  Pallas kernels  129 us (93%)
  matrix products  3.17 us (2%)
  local copies, waits for them, and re-layouts  2.22 us (2%)
  between operations  1.86 us (1%)
    pallas_call x1, Pallas kernels, filter_call(): pl.pallas_call(functools.partial(filter_kernel, groups), out_shape=jax.Sh...  83.5 us
    pallas_call x1, Pallas kernels, inverse_factor(): pl.pallas_call(functools.partial(orthogonal_kernel, nb, width * slabs * b...  45.4 us
    dot_general x1, matrix products, local(): return jnp.dot(factor_inverse, grid_layout, precision=lax.Precision.HIGH)  3.17 us

profile of v3, /device:TPU:1, one launch (start us, length us, event | category | flops | bytes accessed | tf_op | source)
XLA Modules:
  0.0 136.2 jit_solution(16940295379254462807)
XLA Ops:
  1.8 0.6 stack.48.scal_ref
  2.5 83.5 %cheb_filter.1 = f32[8,64,1024]{2,1,0:T(8,128)} custom-call(s32[8]{0:T(128)} %plane_ref.1, s32[8]{0:T(128)} %kind_ref.1, f32[13]{0:T(128)} %stack.48.scal_ref, f32[64,16,512]{2,1,0:T(8,128)} %orb_ref.1, f32[16,512]{1,0:T(8,128)} %pot_ref.1, f32[8,128]{1,0:T(8,128)} %coef_ref.1, f32[4,2048,128]{2,1,0:T(8,128)} %proj_ref.1), custom_call_target="tpu_custom_call" | custom-call | tf_op jit(solution)/shard_map/cheb_filter/pallas_call | solution.py:331
  86.0 0.0 copy-start
  86.0 1.6 %copy-done = f32[8,64,1024]{2,1,0:T(8,128)S(1)} copy-done((f32[8,64,1024]{2,1,0:T(8,128)S(1)}, f32[8,64,1024]{2,1,0:T(8,128)}, u32[]{:S(2)}) %copy-start) | copy-done | bytes 2097176
  87.6 45.4 %gram_factor.1 = f32[512,512]{1,0:T(8,128)S(1)} custom-call(f32[512,1024]{1,0:T(8,128)S(1)} %bitcast.16), custom_call_target="tpu_custom_call" | custom-call | tf_op jit(solution)/shard_map/gram_factor/pallas_call | solution.py:561
  133.0 3.2 %fusion = f32[512,1024]{1,0:T(8,128)} fusion(f32[512,512]{1,0:T(8,128)S(1)} %gram_factor.1, f32[512,1024]{1,0:T(8,128)S(1)} %bitcast.17), kind=kOutput, calls=%fused_computation | convolution fusion | flops 1610612736 | bytes 5242880 | tf_op jit(solution)/shard_map/dot_general | solution.py:605
Async XLA Ops:
  86.0 1.6 %copy-start = (f32[8,64,1024]{2,1,0:T(8,128)S(1)}, f32[8,64,1024]{2,1,0:T(8,128)}, u32[]{:S(2)}) copy-start(f32[8,64,1024]{2,1,0:T(8,128)} %cheb_filter.1) | copy-start | bytes 6291460

commit v4 on v3

--- a/solution.py
+++ b/solution.py
@@ -68,7 +68,6 @@
         pl.semaphore_signal(barrier, inc=1, device_id={"slab": neighbour}, device_id_type=MESH)
     for d in range(1, bands):
         pl.semaphore_signal(barrier, inc=1, device_id={"band": lax.rem(my_band + d, bands)}, device_id_type=MESH)
-    pl.semaphore_wait(barrier, bands + 1)
 
     zeros = jnp.zeros((rows, points), f32)
 
@@ -156,6 +155,7 @@
                 )
         return found
 
+    pl.semaphore_wait(barrier, bands + 1)
     for g in range(groups):
         for copy in copies_from(even, g, 0, None):
             copy.start()
@@ -237,23 +237,23 @@
             seat_of = [pairs[0, a] for a in range(atoms)]
             slots = {x: [jnp.clip(x - places[a], -1, depth) + 1 for a in range(atoms)] for x in range(planes)}
 
-            def quads(xs, take, before=None, after=None):
-                both = jnp.concatenate([split[x] for x in xs], axis=0)
+            def quads(xs, take, first_row, count):
+                both = jnp.concatenate(
+                    [split[x, base + first_row : base + first_row + count] for x in xs for base in (0, share)], axis=0
+                )
                 r = jnp.dot(both, lap[...], preferred_element_type=f32)
                 piece = min(16, share)
                 span = min(256, points)
-                for r0, l0 in [(r0, l0) for r0 in range(0, share, piece) for l0 in range(0, points, span)]:
+                for r0, l0 in [(r0, l0) for r0 in range(first_row, first_row + count, piece) for l0 in range(0, points, span)]:
                     ls = slice(l0, l0 + span)
-                    if before is not None and r0 % half == 0 and l0 == 0:
-                        before(r0 // half)
                     fs = {}
                     for x in xs:
                         for d in (-2, -1, 0, 1, 2):
                             if x + d not in fs:
                                 fs[x + d] = take(x + d, r0, piece, ls)
                     for i, x in enumerate(xs):
-                        base = i * 2 * share + r0
-                        total = (r[base : base + piece, ls] + r[base + share : base + share + piece, ls]) * (-0.5 / 12.0)
+                        base = i * 2 * count + r0 - first_row
+                        total = (r[base : base + piece, ls] + r[base + count : base + count + piece, ls]) * (-0.5 / 12.0)
                         total = total + (pot_ref[pl.ds(x, 1), ls] + (1.25 - centre)) * fs[x]
                         total = total + (fs[x - 1] + fs[x + 1]) * (-2.0 / 3.0) + (fs[x - 2] + fs[x + 2]) * (1.0 / 24.0)
                         for a in range(atoms):
@@ -264,8 +264,6 @@
                         high, low = halves(fresh)
                         split[x, r0 : r0 + piece, ls] = high
                         split[x, share + r0 : share + r0 + piece, ls] = low
-                    if after is not None and (r0 + piece) % half == 0 and l0 + span == points:
-                        after(r0 // half)
 
             def take(x, r0, piece, ls):
                 if x < 0:
@@ -274,9 +272,6 @@
                     return halo[g, s, 1, r0 // half, x - planes, r0 % half : r0 % half + piece, ls]
                 return cur[x, pl.ds(first + r0, piece), ls]
 
-            for x0 in range(2, planes - 2, quad):
-                quads(list(range(x0, min(x0 + quad, planes - 2))), take)
-
             def before(h):
                 for copy in copies_from(cur, g, s, h):
                     copy.wait()
@@ -287,7 +282,13 @@
                     for copy in copies_from(nxt, g, s + 1, h):
                         copy.start()
 
-            quads([0, 1, planes - 2, planes - 1], take, before, after)
+            for h in range(share // half):
+                before(h)
+                quads([0, 1, planes - 2, planes - 1], take, h * half, half)
+                after(h)
+                if h == 0:
+                    for x0 in range(2, planes - 2, quad):
+                        quads(list(range(x0, min(x0 + quad, planes - 2))), take, 0, share)
 
         def two(i, c):
             step(2 * i, even, odd)
@@ -401,7 +402,7 @@
         t_ref[k : k + micro, :] = jnp.where(lanes < k + micro, final, 0.0)
 
 
-def factor_body(nb, a_ref, w_ref, t_ref, cols_ref):
+def factor_body(nb, a_ref, w_ref, t_ref, cols_ref, complete):
     n = w_ref.shape[0]
     nt = (((1,), (1,)), ((), ()))
     count = n // nb
@@ -410,6 +411,7 @@
         at = pl.ds(pl.multiple_of(b * nb, nb), nb)
         t_ref[...] = a_ref[at, at]
         invert_block(t_ref, cols_ref, nb)
+        pl.when(b == 0)(complete)
         for i in range(count):
 
             @pl.when(b == i)
@@ -439,16 +441,13 @@
 ):
     n = w_ref.shape[0]
     count = n // nb
-    total = pack.shape[0]
     slabs, bands = lax.axis_size("slab"), lax.axis_size("band")
     my_slab, my_band = lax.axis_index("slab"), lax.axis_index("band")
     lines = slabs // 2
     chips = bands * lines
     core, chip = lax.rem(my_slab, 2), my_band * lines + my_slab // 2
     partner = my_slab + 1 - 2 * core
-    deep = total // 2
-    thin = deep // chips
-    base = core * deep
+    sections = gram_sections(count, nb, chips)
 
     barrier = pltpu.get_barrier_semaphore()
 
@@ -468,51 +467,21 @@
         high, low = halves(f_ref[rows, :])
         stack[i, :nb] = high
         stack[i, nb:] = low
-    at = 0
-    for j in range(count):
-        for i in range(j, count):
+    for start, size, blocks in sections:
+        at = start
+        for i, j in blocks:
             r = lax.dot_general(stack[i], stack[j], (((1,), (1,)), ((), ())), preferred_element_type=f32)
             r = (r[:nb, :nb] + r[nb:, nb:]) + (r[:nb, nb:] + r[nb:, :nb])
             pack[at : at + nb] = r * (1.0 / point_total)
             at += nb
-    if at < total:
-        pack[at:] = jnp.zeros((total - at, nb), f32)
+        if at < start + size:
+            pack[at : start + size] = jnp.zeros((start + size - at, nb), f32)
+    a_ref[...] = jnp.zeros((n, n), f32)
 
     pl.semaphore_wait(barrier, chips)
 
     def span(start, length):
         return pl.ds(pl.multiple_of(start, 8), length)
-
-    swap = pltpu.make_async_remote_copy(
-        src_ref=pack.at[span((1 - core) * deep, deep)], dst_ref=first, send_sem=pair_sems.at[0],
-        recv_sem=pair_sems.at[1], device_id={"slab": partner}, device_id_type=MESH,
-    )
-    swap.start()
-    swap.wait()
-    part[...] = pack[span(base, deep)] + first[...]
-
-    def scatter(d):
-        other, device = place(d)
-        return pltpu.make_async_remote_copy(
-            src_ref=part.at[span(other * thin, thin)], dst_ref=second.at[d - 1], send_sem=sum_send.at[d - 1],
-            recv_sem=sum_recv.at[d - 1], device_id=device, device_id_type=MESH,
-        )
-
-    def mine(c):
-        return span(base + c * thin, thin)
-
-    def gather(d):
-        return pltpu.make_async_remote_copy(
-            src_ref=full.at[mine(chip)], dst_ref=full.at[mine(chip)], send_sem=gather_send.at[d - 1],
-            recv_sem=gather_recv.at[d - 1], device_id=place(d)[1], device_id_type=MESH,
-        )
-
-    def relay(d):
-        rows = mine(lax.rem(chip + chips - d, chips))
-        return pltpu.make_async_remote_copy(
-            src_ref=full.at[rows], dst_ref=full.at[rows], send_sem=relay_send.at[d], recv_sem=relay_recv.at[d],
-            device_id={"slab": partner}, device_id_type=MESH,
-        )
 
     def each(first_index, action):
         def body(d, c):
@@ -521,30 +490,110 @@
 
         lax.fori_loop(first_index, chips, body, 0)
 
-    each(1, lambda d: scatter(d).start())
-    each(1, lambda d: scatter(d).wait())
-
-    def accumulate(d, value):
-        return value + second[d - 1]
-
-    full[mine(chip)] = lax.fori_loop(1, chips, accumulate, part[span(chip * thin, thin)])
-    each(1, lambda d: gather(d).start())
-    relay(0).start()
-
-    def pass_on(d):
-        gather(d).wait()
-        relay(d).start()
-
-    each(1, pass_on)
-    each(0, lambda d: relay(d).wait())
-
-    a_ref[...] = jnp.zeros((n, n), f32)
-    at = 0
-    for j in range(count):
-        for i in range(j, count):
-            a_ref[i * nb : (i + 1) * nb, j * nb : (j + 1) * nb] = full[at : at + nb]
-            at += nb
-    factor_body(nb, a_ref, w_ref, t_ref, cols_ref)
+    class Section:
+        def __init__(self, index):
+            self.index = index
+            start, size, self.blocks = sections[index]
+            self.start, self.deep = start, size // 2
+            self.thin = self.deep // chips
+            self.low = start // 2
+            self.base = start + core * self.deep
+            self.row = sum(sections[i][1] for i in range(index)) // 2 // chips
+
+        def swap(self):
+            return pltpu.make_async_remote_copy(
+                src_ref=pack.at[span(self.start + (1 - core) * self.deep, self.deep)],
+                dst_ref=first.at[pl.ds(self.low, self.deep)],
+                send_sem=pair_sems.at[self.index, 0], recv_sem=pair_sems.at[self.index, 1],
+                device_id={"slab": partner}, device_id_type=MESH,
+            )
+
+        def combine(self):
+            own = pl.ds(self.low, self.deep)
+            part[own] = pack[span(self.base, self.deep)] + first[own]
+
+        def scatter(self, d):
+            other, device = place(d)
+            return pltpu.make_async_remote_copy(
+                src_ref=part.at[span(self.low + other * self.thin, self.thin)],
+                dst_ref=second.at[d - 1, self.row : self.row + self.thin],
+                send_sem=sum_send.at[self.index, d - 1], recv_sem=sum_recv.at[self.index, d - 1],
+                device_id=device, device_id_type=MESH,
+            )
+
+        def mine(self, c):
+            return span(self.base + c * self.thin, self.thin)
+
+        def total(self):
+            def accumulate(d, value):
+                return value + second[d - 1, self.row : self.row + self.thin]
+
+            full[self.mine(chip)] = lax.fori_loop(
+                1, chips, accumulate, part[span(self.low + chip * self.thin, self.thin)]
+            )
+
+        def gather(self, d):
+            return pltpu.make_async_remote_copy(
+                src_ref=full.at[self.mine(chip)], dst_ref=full.at[self.mine(chip)],
+                send_sem=gather_send.at[self.index, d - 1], recv_sem=gather_recv.at[self.index, d - 1],
+                device_id=place(d)[1], device_id_type=MESH,
+            )
+
+        def relay(self, d):
+            rows = self.mine(lax.rem(chip + chips - d, chips))
+            return pltpu.make_async_remote_copy(
+                src_ref=full.at[rows], dst_ref=full.at[rows], send_sem=relay_send.at[self.index, d],
+                recv_sem=relay_recv.at[self.index, d], device_id={"slab": partner}, device_id_type=MESH,
+            )
+
+        def publish(self):
+            self.total()
+            each(1, lambda d: self.gather(d).start())
+            self.relay(0).start()
+
+        def finish(self):
+            def pass_on(d):
+                self.gather(d).wait()
+                self.relay(d).start()
+
+            each(1, pass_on)
+            each(0, lambda d: self.relay(d).wait())
+            at = self.start
+            for i, j in self.blocks:
+                a_ref[i * nb : (i + 1) * nb, j * nb : (j + 1) * nb] = full[at : at + nb]
+                at += nb
+
+    parts = [Section(index) for index in range(len(sections))]
+    for section in parts:
+        section.swap().start()
+    for section in parts:
+        section.swap().wait()
+        section.combine()
+        each(1, lambda d: section.scatter(d).start())
+    for section in parts:
+        each(1, lambda d: section.scatter(d).wait())
+        section.publish()
+    parts[0].finish()
+
+    def complete():
+        for section in parts[1:]:
+            section.finish()
+
+    factor_body(nb, a_ref, w_ref, t_ref, cols_ref, complete)
+
+
+def gram_sections(count, nb, chips):
+    unit = 16 * chips
+    found, start = [], 0
+    for blocks in (
+        [(i, 0) for i in range(count)],
+        [(i, j) for j in range(1, count) for i in range(j, count)],
+    ):
+        size = (len(blocks) * nb + unit - 1) // unit * unit
+        if blocks:
+            found.append((start, size, blocks))
+            start += size
+    return found
 
 
 def inverse_factor(grid_layout):
@@ -553,9 +602,9 @@
     slabs, bands = lax.axis_size("slab"), lax.axis_size("band")
     chips = bands * slabs // 2
     count = n // nb
-    used = count * (count + 1) // 2 * nb
-    unit = 16 * chips
-    total = (used + unit - 1) // unit * unit
+    sections = gram_sections(count, nb, chips)
+    total = sum(size for _, size, _ in sections)
+    parts = len(sections)
     vmem = pl.BlockSpec(memory_space=pltpu.VMEM)
     dma = pltpu.SemaphoreType.DMA
     return pl.pallas_call(
@@ -573,13 +622,13 @@
             pltpu.VMEM((n, n), f32),
             pltpu.VMEM((nb, nb), f32),
             pltpu.VMEM((micro, micro, nb), f32),
-            dma((2,)),
-            dma((chips - 1,)),
-            dma((chips - 1,)),
-            dma((chips - 1,)),
-            dma((chips - 1,)),
-            dma((chips,)),
-            dma((chips,)),
+            dma((parts, 2)),
+            dma((parts, chips - 1)),
+            dma((parts, chips - 1)),
+            dma((parts, chips - 1)),
+            dma((parts, chips - 1)),
+            dma((parts, chips)),
+            dma((parts, chips)),
         ],
         compiler_params=pltpu.CompilerParams(
             collective_id=1, has_side_effects=True, vmem_limit_bytes=32 * 1024 * 1024

time: 138 us -> 133 us (0.964)
  Pallas kernels: 129 us -> 125 us
    pallas_call x1, Pallas kernels: 45.4 us -> 43 us  [inverse_factor(): pl.pallas_call(functools.partial(orthogonal_kernel, nb, width * slabs * b...]
    pallas_call x1, Pallas kernels: 83.5 us -> 81.7 us  [filter_call(): pl.pallas_call(functools.partial(filter_kernel, groups), out_shape=jax.Sh...]
where the time goes in v4:
time: 133 us; the launch traced here: 132 us
  Pallas kernels  125 us (94%)
  matrix products  3.17 us (2%)
  local copies, waits for them, and re-layouts  2.22 us (2%)
  between operations  1.86 us (1%)
    pallas_call x1, Pallas kernels, filter_call(): pl.pallas_call(functools.partial(filter_kernel, groups), out_shape=jax.Sh...  81.7 us
    pallas_call x1, Pallas kernels, inverse_factor(): pl.pallas_call(functools.partial(orthogonal_kernel, nb, width * slabs * b...  43 us
    dot_general x1, matrix products, local(): return jnp.dot(factor_inverse, grid_layout, precision=lax.Precision.HIGH)  3.17 us

profile of v4, /device:TPU:1, one launch (start us, length us, event | category | flops | bytes accessed | tf_op | source)
XLA Modules:
  0.0 131.9 jit_solution(7547510638614402657)
XLA Ops:
  1.8 0.6 stack.48.scal_ref
  2.5 81.7 %cheb_filter.1 = f32[8,64,1024]{2,1,0:T(8,128)} custom-call(s32[8]{0:T(128)} %plane_ref.1, s32[8]{0:T(128)} %kind_ref.1, f32[13]{0:T(128)} %stack.48.scal_ref, f32[64,16,512]{2,1,0:T(8,128)} %orb_ref.1, f32[16,512]{1,0:T(8,128)} %pot_ref.1, f32[8,128]{1,0:T(8,128)} %coef_ref.1, f32[4,2048,128]{2,1,0:T(8,128)} %proj_ref.1), custom_call_target="tpu_custom_call" | custom-call | tf_op jit(solution)/shard_map/cheb_filter/pallas_call | solution.py:332
  84.2 0.0 copy-start
  84.2 1.6 %copy-done = f32[8,64,1024]{2,1,0:T(8,128)S(1)} copy-done((f32[8,64,1024]{2,1,0:T(8,128)S(1)}, f32[8,64,1024]{2,1,0:T(8,128)}, u32[]{:S(2)}) %copy-start) | copy-done | bytes 2097176
  85.8 43.0 %gram_factor.1 = f32[512,512]{1,0:T(8,128)S(1)} custom-call(f32[512,1024]{1,0:T(8,128)S(1)} %bitcast.16), custom_call_target="tpu_custom_call" | custom-call | tf_op jit(solution)/shard_map/gram_factor/pallas_call | solution.py:610
  128.8 3.2 %fusion = f32[512,1024]{1,0:T(8,128)} fusion(f32[512,512]{1,0:T(8,128)S(1)} %gram_factor.1, f32[512,1024]{1,0:T(8,128)S(1)} %bitcast.17), kind=kOutput, calls=%fused_computation | convolution fusion | flops 1610612736 | bytes 5242880 | tf_op jit(solution)/shard_map/dot_general | solution.py:654
Async XLA Ops:
  84.2 1.6 %copy-start = (f32[8,64,1024]{2,1,0:T(8,128)S(1)}, f32[8,64,1024]{2,1,0:T(8,128)}, u32[]{:S(2)}) copy-start(f32[8,64,1024]{2,1,0:T(8,128)} %cheb_filter.1) | copy-start | bytes 6291460

commit v5 on v4

--- a/solution.py
+++ b/solution.py
@@ -40,8 +40,8 @@
 
 
 def filter_kernel(
-    groups, plane_ref, kind_ref, scal_ref, orb_ref, pot_ref, coef_ref, proj_ref,
-    out_ref, table, back, lap, even, odd, split, spread, halo, raw, pairs, load_sem, table_sem, own_sem,
+    groups, plane_ref, kind_ref, cut_ref, top_ref, orb_ref, pot_ref, coef_ref, proj_ref,
+    out_ref, table, back, lap, even, odd, split, spread, halo, raw, pairs, scal_ref, load_sem, table_sem, own_sem,
     send_sem, recv_sem, out_sem, in_sem,
 ):
     rows, planes, points = orb_ref.shape
@@ -54,14 +54,14 @@
     me, my_band = lax.axis_index("slab"), lax.axis_index("band")
     right, left = lax.rem(me + 1, slabs), lax.rem(me + slabs - 1, slabs)
 
+    tables = []
+    for k in range(kinds):
+        tables.append(pltpu.make_async_copy(proj_ref.at[k], raw.at[k], table_sem.at[k]))
+        tables[-1].start()
     loads = []
     for x in range(planes):
         loads.append(pltpu.make_async_copy(orb_ref.at[:, x], even.at[x], load_sem.at[x]))
         loads[-1].start()
-    tables = []
-    for k in range(kinds):
-        tables.append(pltpu.make_async_copy(proj_ref.at[k], raw.at[k], table_sem.at[k]))
-        tables[-1].start()
 
     barrier = pltpu.get_barrier_semaphore()
     for neighbour in (left, right):
@@ -119,6 +119,11 @@
 
     for copy in loads:
         copy.wait()
+
+    centre, steps = chebyshev_scalars(cut_ref[0], top_ref[0])
+    for i, (scale, pull) in enumerate(steps):
+        scal_ref[2 * i] = scale
+        scal_ref[2 * i + 1] = jnp.float32(0.0) if pull is None else pull
 
     slot_count = pair_slots(atoms, kinds)
     kind_of = [jnp.clip(kind_ref[a], 0, kinds - 1) for a in range(atoms)]
@@ -160,7 +165,6 @@
         for copy in copies_from(even, g, 0, None):
             copy.start()
 
-    centre = scal_ref[2 * ORDER]
     quad = 4
     places = [plane_ref[a] - me * planes for a in range(atoms)]
     order = sorted(range(1, bands), key=lambda d: abs(d - bands / 2))
@@ -315,7 +319,7 @@
         own(u).wait()
 
 
-def filter_call(plane, kind, scal, orb, pot, coef, proj, groups):
+def filter_call(plane, kind, cut, top, orb, pot, coef, proj, groups):
     rows, planes, points = orb.shape
     atoms = coef.shape[0]
     kinds, block, funcs = proj.shape
@@ -332,7 +336,7 @@
     return pl.pallas_call(
         functools.partial(filter_kernel, groups),
         out_shape=jax.ShapeDtypeStruct((bands, rows, planes * points // bands), f32),
-        in_specs=[smem] * 3 + [hbm, vmem, vmem, hbm],
+        in_specs=[smem] * 4 + [hbm, vmem, vmem, hbm],
         out_specs=vmem,
         scratch_shapes=[
             pltpu.VMEM((kinds, block, 2 * funcs), bf16),
@@ -345,6 +349,7 @@
             pltpu.VMEM((groups, ORDER, 2, share // half, 2, half, points), f32),
             pltpu.VMEM((kinds, block, funcs), f32),
             pltpu.SMEM((2, max(atoms, 2 * pair_slots(atoms, kinds))), jnp.int32),
+            pltpu.SMEM((2 * ORDER,), f32),
             dma((planes,)),
             dma((kinds,)),
             dma((units,)),
@@ -357,7 +362,7 @@
             collective_id=0, has_side_effects=True, vmem_limit_bytes=60 * 1024 * 1024
         ),
         name="cheb_filter",
-    )(plane, kind, scal, orb, pot, coef, proj)
+    )(plane, kind, cut, top, orb, pot, coef, proj)
 
 
 def invert_block(t_ref, cols_ref, nb):
@@ -641,13 +646,8 @@
     orbitals, potential, projectors, atom_kind, atom_plane, atom_coef, filter_cut, filter_top
 ):
     rows = orbitals.shape[0]
-    centre, pairs = chebyshev_scalars(filter_cut[0], filter_top[0])
-    scal = []
-    for a, b in pairs:
-        scal += [a, jnp.zeros((), f32) if b is None else b]
-    scal = jnp.stack(scal + [centre])
     filtered = filter_call(
-        atom_plane, atom_kind, scal, orbitals, potential, atom_coef, projectors, 2 if rows % 32 == 0 else 1
+        atom_plane, atom_kind, filter_cut, filter_top, orbitals, potential, atom_coef, projectors, 2 if rows % 32 == 0 else 1
     )
     grid_layout = filtered.reshape(-1, filtered.shape[2])
     factor_inverse = inverse_factor(grid_layout)

time: 133 us -> 131 us (0.985)
  no operation moved by 1% of the time
where the time goes in v5:
time: 131 us; the launch traced here: 130 us
  Pallas kernels  124 us (95%)
  matrix products  3.17 us (2%)
  local copies, waits for them, and re-layouts  1.58 us (1%)
  between operations  1.32 us (1%)
    pallas_call x1, Pallas kernels, filter_call(): pl.pallas_call(functools.partial(filter_kernel, groups), out_shape=jax.Sh...  81.2 us
    pallas_call x1, Pallas kernels, inverse_factor(): pl.pallas_call(functools.partial(orthogonal_kernel, nb, width * slabs * b...  43 us
    dot_general x1, matrix products, local(): return jnp.dot(factor_inverse, grid_layout, precision=lax.Precision.HIGH)  3.17 us

profile of v5, /device:TPU:1, one launch (start us, length us, event | category | flops | bytes accessed | tf_op | source)
XLA Modules:
  0.0 130.3 jit_solution(4633390001813224710)
XLA Ops:
  1.3 81.2 %cheb_filter.1 = f32[8,64,1024]{2,1,0:T(8,128)} custom-call(s32[8]{0:T(128)} %plane_ref.1, s32[8]{0:T(128)} %kind_ref.1, f32[1]{0:T(128)S(6)} %copy.9.cut_ref, f32[1]{0:T(128)S(6)} %copy.10.top_ref, f32[64,16,512]{2,1,0:T(8,128)} %orb_ref.1, f32[16,512]{1,0:T(8,128)} %pot_ref.1, f32[8,128]{1,0:T(8,128)} %coef_ref.1, f32[4,2048,128]{2,1,0:T(8,128)} %proj_ref.1), custom_call_target="tpu_custom_call" | custom-call | tf_op jit(solution)/shard_map/cheb_filter/pallas_call | solution.py:336
  82.5 0.0 copy-start
  82.5 1.6 %copy-done = f32[8,64,1024]{2,1,0:T(8,128)S(1)} copy-done((f32[8,64,1024]{2,1,0:T(8,128)S(1)}, f32[8,64,1024]{2,1,0:T(8,128)}, u32[]{:S(2)}) %copy-start) | copy-done | bytes 2097176
  84.1 43.0 %gram_factor.1 = f32[512,512]{1,0:T(8,128)S(1)} custom-call(f32[512,1024]{1,0:T(8,128)S(1)} %bitcast.3), custom_call_target="tpu_custom_call" | custom-call | tf_op jit(solution)/shard_map/gram_factor/pallas_call | solution.py:615
  127.1 3.2 %fusion = f32[512,1024]{1,0:T(8,128)} fusion(f32[512,512]{1,0:T(8,128)S(1)} %gram_factor.1, f32[512,1024]{1,0:T(8,128)S(1)} %bitcast.4), kind=kOutput, calls=%fused_computation | convolution fusion | flops 1610612736 | bytes 5242880 | tf_op jit(solution)/shard_map/dot_general | solution.py:654
Async XLA Ops:
  82.5 1.6 %copy-start = (f32[8,64,1024]{2,1,0:T(8,128)S(1)}, f32[8,64,1024]{2,1,0:T(8,128)}, u32[]{:S(2)}) copy-start(f32[8,64,1024]{2,1,0:T(8,128)} %cheb_filter.1) | copy-start | bytes 6291460
